TPU v7x, 32 devices: a whole 2x2x4 slice. The times are simulated.
32 devices in a mesh: dp: 4 (over y, x), tensor: 2 (over core), precond: 4 (over z).
Axes of the slice: x: 2, y: 2, z: 4, core: 2. Of those that a mesh axis runs over, the one named last changes fastest.
Arguments:
- tokens: bfloat16 [512, 8192], P('dp', 'tensor'), may hold values from -6 to 6
- gain: bfloat16 [8192], P('tensor'), may hold values from 0.099609375 to 1.8984375
- cotangent: bfloat16 [512, 12288], P('dp', 'precond'), may hold values from -6 to 6
Outputs:
- preconditioner: float32 [8, 1024, 1024], P('tensor', ('dp', 'precond'))
All inputs are finite; a program needn't handle non-finite values.
Results may differ from a plain program's by a relative error of at most 0.00089.
Values sent between devices are 32-bit elements; how exact they have to be, the bound alone decides.
No kernel may reach another device: no remote copies, remote signals or barrier semaphores. Data moves between devices by JAX's collectives and lax.ppermute only.
A program may use at most 128 MiB of HBM per device.

v0:
```python
import jax
import jax.numpy as jnp
from jax import lax
from jax.sharding import PartitionSpec as P

BLK = 1024


highest = lax.Precision.HIGHEST
epsilon = 1e-06
damping = 0.01


def batched(left_side, right_side):
    return jnp.einsum("bij,bjk->bik", left_side, right_side, precision=highest)


def body(tokens, gain, cotangent):
    values = tokens.astype(jnp.float32)
    square_part = jnp.sum(values * values, axis=1)[None, :]
    gathered = lax.all_gather(square_part, "tensor", axis=0, tiled=True)
    mean_square = jnp.sum(gathered, axis=0)[:, None] / (values.shape[1] * lax.axis_size("tensor"))
    normed = (values * lax.rsqrt(mean_square + epsilon) * gain.astype(jnp.float32)).astype(
        jnp.bfloat16
    )
    token_total = tokens.shape[0] * lax.axis_size("dp")
    partial_value = lax.dot_general(
        normed, cotangent, (((0,), (0,)), ((), ())), preferred_element_type=jnp.float32
    )
    gradient = lax.psum_scatter(partial_value, "dp", scatter_dimension=1, tiled=True) / token_total
    block_count = gradient.shape[0] // BLK
    blocks = gradient.reshape(block_count, BLK, gradient.shape[1])
    local_gram = jnp.einsum("bik,bjk->bij", blocks, blocks, precision=highest)
    identity = jnp.eye(BLK, dtype=jnp.float32)
    summed_gram = lax.psum(local_gram, ("dp", "precond"))
    statistic = summed_gram + damping * identity
    scaling = 2.0 * jnp.trace(statistic, axis1=1, axis2=2)[:, None, None] / BLK
    start_iterate = statistic / scaling
    factor_one = (5.0 * identity - start_iterate) / 4.0
    row_count = BLK // (lax.axis_size("dp") * lax.axis_size("precond"))
    offset = (
        lax.axis_index("dp") * lax.axis_size("precond") + lax.axis_index("precond")
    ) * row_count
    factor_rows = lax.dynamic_slice_in_dim(factor_one, offset, row_count, 1)
    power_two = batched(factor_rows, factor_one)
    power_three = batched(power_two, factor_one)
    power_four = batched(power_three, factor_one)
    power_five = batched(power_four, factor_one)
    product = batched(power_five, start_iterate)
    return jnp.power(scaling, -0.25) * (5.0 * factor_rows - product) / 4.0


def solution(mesh):
    in_specs = (P("dp", "tensor"), P("tensor"), P("dp", "precond"))
    out_specs = P("tensor", ("dp", "precond"), None)
    return jax.shard_map(body, mesh=mesh, in_specs=in_specs, out_specs=out_specs, check_vma=False)
```

profile of v0, /device:TPU:0, one launch (start us, length us, event | category | flops | bytes accessed | tf_op | source)
XLA Modules:
  0.0 1049.3 jit_solution(3601064974182051058)
XLA Ops:
  6.5 0.0 copy-start
  6.5 0.0 reduce-scatter.2.cloned.1.call-start
  6.5 0.8 convert_element_type.11
  7.3 1.5 fusion.2
  8.8 2.0 all-gather.1
  10.8 20.7 %fusion.7 = f32[4096,3072]{1,0:T(8,128)} fusion(bf16[128,3072]{1,0:T(8,128)(2,1)S(1)} %copy-done, bf16[128,4096]{1,0:T(8,128)(2,1)} %param.3, f32[4096]{0:T(1024)S(1)} %convert_element_type.11, f32[128]{0:T(128)S(1)} %add_rsqrt_fusion), kind=kOutput, calls=%fused_computation.15 | convolution fusion | flops 3223322624 | bytes 52183552 | tf_op jit(solution)/shard_map/dot_general | solution.py:27
  31.5 0.0 reduce-scatter.2.cloned.1.call-update
  31.6 0.0 all-reduce.2.cloned.1.call-start
  31.6 426.7 %reduce-scatter.2.cloned.1.call-done = f32[4096,768]{1,0:T(8,128)} async-done(((f32[4096,3072]{1,0:T(8,128)}), f32[4096,768]{1,0:T(8,128)}) %reduce-scatter.2.cloned.1.call-update) | async-done | bytes 12582928 | tf_op jit(solution)/shard_map/reduce_scatter | solution.py:30
  458.3 10.0 broadcast_multiply_fusion
  468.2 47.3 %fusion.14 = f32[4,1024,1024]{2,1,0:T(8,128)} fusion(f32[4,1024,768]{2,1,0:T(8,128)} %bitcast.13), kind=kOutput, calls=%fused_computation.24 | convolution fusion | flops 38654705664 | bytes 29360128 | tf_op jit(solution)/shard_map/bik,bjk->bij/dot_general | solution.py:33
  515.5 0.0 all-reduce.2.cloned.1.call-update
  515.6 0.3 iota_compare_fusion
  515.9 4.3 fusion
  520.2 446.5 %all-reduce.2.cloned.1.call-done = f32[4,1024,1024]{2,1,0:T(8,128)} async-done(((f32[4,1024,1024]{2,1,0:T(8,128)}), f32[4,1024,1024]{2,1,0:T(8,128)}) %all-reduce.2.cloned.1.call-update) | async-done | bytes 16777232 | tf_op jit(solution)/shard_map/psum | solution.py:35
  966.8 10.3 select_reduce_fusion
  977.0 0.0 copy-done.2
  977.0 8.1 subtract_multiply_fusion
  985.2 10.2 fusion.11
  995.4 10.4 fusion.15
  1005.8 10.4 fusion.16
  1016.2 10.3 fusion.17
  1026.5 0.0 copy-start.1
  1026.5 15.7 %fusion.6 = f32[4,64,1024]{2,1,0:T(8,128)} fusion(f32[4,64,1024]{2,1,0:T(8,128)S(1)} %fusion.17, f32[4,1024,1024]{2,1,0:T(8,128)S(1)} %subtract_multiply_fusion, s32[]{:T(128)S(6)} %select_n.9, f32[4]{0:T(128)S(1)} %get-tuple-element.5, f32[4,1024,1024]{2,1,0:T(8,128)} %all-reduce.2.cloned.1.call-done, f32[4]{0:T(128)S(1)} %get-tuple-element.6, ...), kind=kOutput, calls=%fused_computation.14 | convolution fusion | flops 3230662656 | bytes 24117284 | tf_op jit(solution)/shard_map/bij,bjk->bik/dot_general | solution.py:15
  (8 shorter events, 0.1 us)
Async XLA Ops:
  6.5 4.3 copy-start
  6.5 451.7 %reduce-scatter.2.cloned.1.call-start = ((), (), s32[]{:S(2)}) async-start(), calls=%async_computation.1 | async-start | bytes 62914560 | tf_op jit(solution)/shard_map/reduce_scatter | solution.py:30
  31.6 935.2 %all-reduce.2.cloned.1.call-start = ((), (), s32[]{:S(2)}) async-start(), calls=%async_computation.2 | async-start | bytes 33554432 | tf_op jit(solution)/shard_map/psum | solution.py:35
  966.8 10.3 copy-start.2
  966.8 10.3 copy-start.3
  1026.5 15.7 %copy-start.1 = (bf16[128,3072]{1,0:T(8,128)(2,1)S(1)}, bf16[128,3072]{1,0:T(8,128)(2,1)}, u32[]{:S(2)}) copy-start(bf16[128,3072]{1,0:T(8,128)(2,1)} %param.5) | copy-start | bytes 2359300
Sparse Core Ops, SparseCore 0:
  31.7 426.5 reduce-scatter.1
  515.7 451.0 all-reduce.1
where the time goes:
time: 1050 us
  waiting for transfers between devices  873 us (83%)
  matrix products  125 us (12%)
  other arithmetic  35.3 us (3%)
  between operations  13.8 us (1%)
    psum x1, waiting for transfers between devices, body(): summed_gram = lax.psum(local_gram, ('dp', 'precond'))  447 us
    reduce_scatter x1, waiting for transfers between devices, body(): lax.psum_scatter(partial_value, 'dp', scatter_dimension=1, tiled=True)  427 us
    dot_general x5, matrix products, batched(): return jnp.einsum('bij,bjk->bik', left_side, right_side, precision=highest)  57 us
    dot_general x1, matrix products, body(): local_gram = jnp.einsum('bik,bjk->bij', blocks, blocks, precision=highest)  47.3 us
  transfers between devices with their start and end apart: 2, of which 2 were waited for; matrix products, arithmetic and copies ran while one was open for 0% of the time, Pallas kernels for 0%

commit v1 on v0

v1 whole, which is shorter than its diff:
```python
import functools

import jax
import jax.numpy as jnp
from jax import lax
from jax.experimental import pallas as pl
from jax.experimental.pallas import tpu as pltpu
from jax.sharding import PartitionSpec as P

BLK = 1024

epsilon = 1e-06
damping = 0.01

f32 = jnp.float32
bf16 = jnp.bfloat16
VMEM = pl.BlockSpec(memory_space=pltpu.VMEM)
SMEM = pl.BlockSpec(memory_space=pltpu.SMEM)


def shift(value, axis, by):
    size = lax.axis_size(axis)
    return lax.ppermute(value, axis, [(i, (i + by) % size) for i in range(size)])


def call(kernel, outs, *operands, scratch=(), flops=0):
    moved = sum(a.size * a.dtype.itemsize for a in (*operands, *outs))
    return pl.pallas_call(
        kernel,
        out_shape=list(outs),
        in_specs=[SMEM] + [VMEM] * (len(operands) - 1),
        out_specs=[VMEM] * len(outs),
        scratch_shapes=list(scratch),
        cost_estimate=pl.CostEstimate(flops=flops, bytes_accessed=moved, transcendentals=0),
    )(*operands)


def nt(left, right):
    return lax.dot_general(left, right, (((1,), (1,)), ((), ())), preferred_element_type=f32)


def nn(left, right):
    return lax.dot_general(left, right, (((1,), (0,)), ((), ())), preferred_element_type=f32)


def halves(value):
    high = value.astype(bf16)
    return high, (value - high.astype(f32)).astype(bf16)


def product(left, right):
    return nn(left[0], right[0]) + (nn(left[0], right[1]) + nn(left[1], right[0]))


def gram_kernel(dp, nten, where, own, *refs):
    received, outs, whole, packed = refs[: dp - 1], refs[dp - 1 : -2], refs[-2], refs[-1]
    me, ten = where[0], where[1]
    size = own.shape[0]
    whole[pl.ds(pl.multiple_of(me * size, size), size)] = own[...].astype(bf16)
    for by, piece in enumerate(received, 1):
        source = lax.rem(me + dp - by, dp)
        whole[pl.ds(pl.multiple_of(source * size, size), size)] = piece[...].astype(bf16)
    at = 0
    for i in range(dp):
        rows = nt(whole[i * size : (i + 1) * size], whole[i * size :])
        for j in range(dp - i):
            packed[at * size : (at + 1) * size] = rows[:, j * size : (j + 1) * size]
            at += 1
    if at * size < packed.shape[0]:
        packed[at * size :] = jnp.zeros((packed.shape[0] - at * size, size), f32)
    count = outs[0].shape[0]
    for by, out in enumerate(outs):
        target = lax.rem(ten + by, nten)
        out[...] = packed[pl.ds(pl.multiple_of(target * count, 8), count)]


def split_kernel(axis_at, terms, where, *refs):
    parts, outs, total = refs[:terms], refs[terms:-1], refs[-1]
    value = parts[0][...]
    for part in parts[1:]:
        value = value + part[...]
    total[...] = value
    size, count = len(outs), outs[0].shape[0]
    for by, out in enumerate(outs):
        target = lax.rem(where[axis_at] + by, size)
        out[...] = total[pl.ds(pl.multiple_of(target * count, 8), count)]


def join_kernel(axis_at, where, *refs):
    parts, out = refs[:-1], refs[-1]
    size, count = len(parts), parts[0].shape[0]
    for by, part in enumerate(parts):
        source = lax.rem(where[axis_at] + size - by, size)
        out[pl.ds(pl.multiple_of(source * count, 8), count)] = part[...]


def normed_kernel(dp, nb, npre, where, own, *refs):
    received, normed, gram, columns = refs[: dp - 1], refs[-3], refs[-2], refs[-1]
    me, pre = where[0], where[2]
    size = own.shape[0]
    normed[pl.ds(pl.multiple_of(me * size, size), size)] = own[...].astype(bf16)
    for by, piece in enumerate(received, 1):
        source = lax.rem(me + dp - by, dp)
        normed[pl.ds(pl.multiple_of(source * size, size), size)] = piece[...].astype(bf16)
    gram[...] = nt(normed[...], normed[...])
    select = output_rows(dp, nb, npre, me, pre, columns.shape[0], normed.shape[1])
    columns[...] = nt(select.astype(bf16), normed[...]).astype(bf16)


def output_rows(dp, nb, npre, me, pre, count, width):
    each = width // (dp * npre)
    made = lax.broadcasted_iota(jnp.int32, (count, width), 0)
    column = lax.broadcasted_iota(jnp.int32, (count, width), 1)
    target = lax.rem(me, dp // nb) * nb + made // each
    return ((target * npre + pre) * each + lax.rem(made, each) == column).astype(f32)


def root_kernel(dp, nb, npre, nten, where, normed, gram, columns, *refs):
    pieces, out, packed, inner = refs[:nten], refs[nten], refs[nten + 1], refs[nten + 2]
    me, ten, pre = where[0], where[1], where[2]
    count = pieces[0].shape[0]
    for by, piece in enumerate(pieces):
        source = lax.rem(ten + nten - by, nten)
        packed[pl.ds(pl.multiple_of(source * count, 8), count)] = piece[...]
    total = normed.shape[0]
    size, at = total // dp, 0
    for i in range(dp):
        for j in range(i, dp):
            tile = packed[at * size : (at + 1) * size]
            inner[i * size : (i + 1) * size, j * size : (j + 1) * size] = tile
            if j > i:
                inner[j * size : (j + 1) * size, i * size : (i + 1) * size] = tile.T
            at += 1
    tokens_gram = gram[...]
    width = normed.shape[1]
    power = jnp.sum(jnp.sum(inner[...] * tokens_gram, axis=1, keepdims=True), axis=0, keepdims=True)
    scaling = 2.0 * (power / (float(total) * float(total)) / width + damping)
    shared = 1.0 / (scaling * (float(total) * float(total)))
    damp = damping / scaling
    base = (5.0 - damp) / 4.0
    core = halves(inner[...] * shared)
    mixed = halves(product(halves(tokens_gram), core))
    left = columns[...]
    rows = nn(left, core[0]) + nn(left, core[1])

    def step(value, weight):
        return base * value - 0.25 * product(halves(value), mixed) + weight * rows

    weight = 0.25 * damp
    value = step(-rows, weight)
    for _ in range(3):
        weight = weight * base
        value = step(value, weight)
    weight = weight * base
    value = step(value, weight - 1.25)
    root = lax.rsqrt(jnp.sqrt(scaling))
    value = halves(value * (0.25 * root))
    alone = (5.0 * base - damp * base * base * base * base * base) * 0.25 * root
    made = nn(value[0], normed[...]) + nn(value[1], normed[...])
    select = output_rows(dp, nb, npre, me, pre, made.shape[0], width)
    out[...] = made + alone * select


def body(tokens, gain, cotangent):
    dp, nten, npre = (lax.axis_size(name) for name in ("dp", "tensor", "precond"))
    me, ten, pre = (lax.axis_index(name) for name in ("dp", "tensor", "precond"))
    where = jnp.stack([me, ten, pre]).astype(jnp.int32)
    size, width = tokens.shape
    total = size * dp
    nb = width // BLK
    share = dp // nb
    assert nb * BLK == width and share * nb == dp
    hidden = cotangent.shape[1] // (nten * dp)
    assert hidden * nten * dp == cotangent.shape[1]

    def cotangent_part(to):
        return lax.dynamic_slice_in_dim(cotangent, (ten * dp + to) * hidden, hidden, 1)

    cotangents = [cotangent_part(me)]
    for by in range(1, dp):
        cotangents.append(shift(cotangent_part(lax.rem(me + by, dp)).astype(f32), "dp", by))

    values = tokens.astype(f32)
    square = jnp.sum(values * values, axis=1)[None, :]
    square = square + sum(shift(square, "tensor", by) for by in range(1, nten))
    inverse = lax.rsqrt(square[0][:, None] / (width * nten) + epsilon)

    def normed_part(to):
        at = (to // share) * BLK
        part = lax.dynamic_slice_in_dim(tokens, at, BLK, 1).astype(f32)
        scale = lax.dynamic_slice_in_dim(gain, at, BLK, 0).astype(f32)
        return part * inverse * scale

    normed_parts = [normed_part(me)]
    for by in range(1, dp):
        normed_parts.append(shift(normed_part(lax.rem(me + by, dp)), "dp", by))

    tiles = dp * (dp + 1) // 2
    piece = -(-tiles * size // (nten * npre * 8)) * 8
    packed = jax.ShapeDtypeStruct((nten * npre * piece, size), f32)
    part = jax.ShapeDtypeStruct((npre * piece, size), f32)
    small = jax.ShapeDtypeStruct((piece, size), f32)
    parts = call(
        functools.partial(gram_kernel, dp, nten),
        [part] * nten,
        where,
        *cotangents,
        scratch=[pltpu.VMEM((total, hidden), bf16), pltpu.VMEM(packed.shape, f32)],
        flops=tiles * size * size * hidden * 2,
    )
    parts = [parts[0]] + [shift(parts[by], "tensor", by) for by in range(1, nten)]
    pieces = call(
        functools.partial(split_kernel, 2, nten),
        [small] * npre,
        where,
        *parts,
        scratch=[pltpu.VMEM(part.shape, f32)],
    )
    summed = pieces[0] + sum(shift(pieces[by], "precond", by) for by in range(1, npre))
    summed = summed + sum(shift(summed, "dp", by) for by in range(1, dp))
    pieces = [summed] + [shift(summed, "precond", by) for by in range(1, npre)]
    (joined,) = call(functools.partial(join_kernel, 2), [part], where, *pieces)
    parts = [joined] + [shift(joined, "tensor", by) for by in range(1, nten)]

    made = nb * (BLK // (dp * npre))
    normed, gram, columns = call(
        functools.partial(normed_kernel, dp, nb, npre),
        [
            jax.ShapeDtypeStruct((total, BLK), bf16),
            jax.ShapeDtypeStruct((total, total), f32),
            jax.ShapeDtypeStruct((made, total), bf16),
        ],
        where,
        *normed_parts,
        flops=2 * total * total * BLK + 2 * made * BLK * total,
    )
    (rows,) = call(
        functools.partial(root_kernel, dp, nb, npre, nten),
        [jax.ShapeDtypeStruct((made, BLK), f32)],
        where,
        normed,
        gram,
        columns,
        *parts,
        scratch=[pltpu.VMEM(packed.shape, f32), pltpu.VMEM((total, total), f32)],
        flops=2 * total * total * (3 * total + 17 * made),
    )
    rows = rows.reshape(nb, made // nb, BLK)
    if share == 1:
        return lax.all_to_all(rows, "dp", 0, 0, tiled=True)
    block, member = me // share, lax.rem(me, share)
    result = jnp.zeros_like(rows)
    for by in range(nb):
        sent = lax.dynamic_index_in_dim(rows, lax.rem(block + by, nb), 0, True)
        pairs = [(b * share + m, m * nb + (b + by) % nb) for b in range(nb) for m in range(share)]
        if any(a != b for a, b in pairs):
            sent = lax.ppermute(sent, "dp", pairs)
        source = lax.rem(lax.rem(me, nb) + nb - by, nb)
        result = lax.dynamic_update_slice_in_dim(result, sent, source, 0)
    return result


def solution(mesh):
    in_specs = (P("dp", "tensor"), P("tensor"), P("dp", "precond"))
    out_specs = P("tensor", ("dp", "precond"), None)
    return jax.shard_map(body, mesh=mesh, in_specs=in_specs, out_specs=out_specs, check_vma=False)
```

time: 1050 us -> 98.3 us (0.09)
  waiting for transfers between devices: 873 us -> 27.7 us
  matrix products: 125 us -> 0 us
  other arithmetic: 35.3 us -> 4.79 us
  starting transfers between devices: 0.04 us -> 24.7 us
  Pallas kernels: 0 us -> 17.3 us
  blocking collectives: 1.95 us -> 18.6 us
  between operations: 13.8 us -> 0.1 us
    psum x1 -> x0, waiting for transfers between devices: 447 us -> none  [body(): summed_gram = lax.psum(local_gram, ('dp', 'precond'))]
    reduce_scatter x1 -> x0, waiting for transfers between devices: 427 us -> none  [body(): lax.psum_scatter(partial_value, 'dp', scatter_dimension=1, tiled=True)]
    dot_general x7 -> x0, matrix products: 125 us -> none  [the longest x5 57 us: batched(): return jnp.einsum('bij,bjk->bik', left_side, right_side, precision=highest)]
    ppermute x0 -> x18, waiting for transfers between devices: none -> 27.7 us  [shift(): lax.ppermute(value, axis, [(i, (i + by) % size) for i in range(size)])]
    ppermute x0 -> x18, starting transfers between devices: none -> 24.7 us  [shift(): lax.ppermute(value, axis, [(i, (i + by) % size) for i in range(size)])]
    all_to_all x0 -> x1, blocking collectives: none -> 18.6 us  [body(): return lax.all_to_all(rows, 'dp', 0, 0, tiled=True)]
    div x2 -> x0, other arithmetic: 18.1 us -> none  [the longest x1 9.95 us: body(): lax.psum_scatter(partial_value, 'dp', scatter_dimension=1, tiled=True)]
    pallas_call x0 -> x5, Pallas kernels: none -> 17.3 us  [call(): pl.pallas_call(kernel, out_shape=list(outs), in_specs=[SMEM] + [VMEM] * (...]
  transfers between devices with their start and end apart: 2 -> 18, of which waited for: 2 -> 10; matrix products, arithmetic and copies ran while one was open for 0% -> 2% of each run, Pallas kernels for 0% -> 7%
where the time goes in v1:
time: 98.3 us; the launch traced here: 97.9 us
  waiting for transfers between devices  27.7 us (28%)
  starting transfers between devices  24.7 us (25%)
  blocking collectives  18.6 us (19%)
  Pallas kernels  17.3 us (18%)
  other arithmetic  4.79 us (5%)
  local copies, waits for them, and re-layouts  4.72 us (5%)
    ppermute x18, waiting for transfers between devices, shift(): lax.ppermute(value, axis, [(i, (i + by) % size) for i in range(size)])  27.7 us
    ppermute x18, starting transfers between devices, shift(): lax.ppermute(value, axis, [(i, (i + by) % size) for i in range(size)])  24.7 us
    all_to_all x1, blocking collectives, body(): return lax.all_to_all(rows, 'dp', 0, 0, tiled=True)  18.6 us
    pallas_call x5, Pallas kernels, call(): pl.pallas_call(kernel, out_shape=list(outs), in_specs=[SMEM] + [VMEM] * (...  17.3 us
    unnamed x27, local copies, waits for them, and re-layouts  4.72 us
  transfers between devices with their start and end apart: 18, of which 10 were waited for; matrix products, arithmetic and copies ran while one was open for 2% of the time, Pallas kernels for 7%

profile of v1, /device:TPU:0, one launch (start us, length us, event | category | flops | bytes accessed | tf_op | source)
XLA Modules:
  0.0 97.9 jit_solution(14861449913080138567)
XLA Ops:
  0.0 1.8 %dynamic-slice_convert_fusion = (f32[128,384]{1,0:T(8,128)S(1)}, f32[128,384]{1,0:T(8,128)S(1)}, bf16[128,384]{1,0:T(8,128)(2,1)}, f32[128,384]{1,0:T(8,128)S(1)}) fusion(bf16[128,3072]{1,0:T(8,128)(2,1)} %param.5, s32[]{:T(128)S(6)} %select_n.41, s32[]{:T(128)S(6)} %select_n.39, s32[]{:T(128)S(6)} %select_n.38, s32[]{:T(128)S(6)} %select_n.40), kind=kLoop, calls=%fused_computation.5 | loop fusion | flops 147456 | bytes 1081360 | tf_op jit(solution)/shard_map/convert_element_type | solution.py:181
  1.8 3.0 %collective-permute-start.4 = (f32[128,384]{1,0:T(8,128)S(1)}, f32[128,384]{1,0:T(8,128)S(1)}, u32[]{:S(2)}, u32[]{:S(2)}) collective-permute-start(f32[128,384]{1,0:T(8,128)S(1)} %get-tuple-element.28), channel_id=1, source_target_pairs={{0,8},{8,16},{16,24},{24,0},{1,9},{9,17},{17,25},{25,1},{2,10},{10... | collective-permute-start | bytes 589832 | tf_op jit(solution)/shard_map/ppermute | solution.py:23
  4.8 1.5 %collective-permute-start.5 = (f32[128,384]{1,0:T(8,128)S(1)}, f32[128,384]{1,0:T(8,128)S(1)}, u32[]{:S(2)}, u32[]{:S(2)}) collective-permute-start(f32[128,384]{1,0:T(8,128)S(1)} %get-tuple-element.30), channel_id=1, source_target_pairs={{0,16},{8,24},{16,0},{24,8},{1,17},{9,25},{17,1},{25,9},{2,18},{10... | collective-permute-start | bytes 589832 | tf_op jit(solution)/shard_map/ppermute | solution.py:23
  8.3 3.2 %collective-permute-done.4.refs_0_ = f32[128,384]{1,0:T(8,128)S(1)} collective-permute-done((f32[128,384]{1,0:T(8,128)S(1)}, f32[128,384]{1,0:T(8,128)S(1)}, u32[]{:S(2)}, u32[]{:S(2)}) %collective-permute-start.4) | collective-permute-done | bytes 196640 | tf_op jit(solution)/shard_map/ppermute | solution.py:23
  11.5 3.3 %collective-permute-done.5.refs_1_ = f32[128,384]{1,0:T(8,128)S(1)} collective-permute-done((f32[128,384]{1,0:T(8,128)S(1)}, f32[128,384]{1,0:T(8,128)S(1)}, u32[]{:S(2)}, u32[]{:S(2)}) %collective-permute-start.5) | collective-permute-done | bytes 196640 | tf_op jit(solution)/shard_map/ppermute | solution.py:23
  15.8 2.6 %shard_map.38 = (f32[640,128]{1,0:T(8,128)}, f32[640,128]{1,0:T(8,128)}) custom-call(s32[3]{0:T(128)} %pad_add_fusion.where, bf16[128,384]{1,0:T(8,128)(2,1)} %get-tuple-element.29.own, f32[128,384]{1,0:T(8,128)} %copy-done.3, f32[128,384]{1,0:T(8,128)} %copy-done.4, f32[128,384]{1,0:T(8,128)} %copy-done.5), custom_call_target="tpu_custom_call" | custom-call | flops 125829120 | bytes 1343500 | tf_op jit(solution)/shard_map/pallas_call | solution.py:28
  21.0 1.8 %shard_map.39 = (f32[160,128]{1,0:T(8,128)}, f32[160,128]{1,0:T(8,128)}, f32[160,128]{1,0:T(8,128)}, f32[160,128]{1,0:T(8,128)}) custom-call(s32[3]{0:T(128)} %pad_add_fusion.where, f32[640,128]{1,0:T(8,128)} %get-tuple-element.17.refs_0_, f32[640,128]{1,0:T(8,128)} %copy-done.2), custom_call_target="tpu_custom_call" | custom-call | bytes 983052 | tf_op jit(solution)/shard_map/pallas_call | solution.py:28
  22.8 3.6 %collective-permute-start.10 = (f32[160,128]{1,0:T(8,128)}, f32[160,128]{1,0:T(8,128)S(1)}, u32[]{:S(2)}, u32[]{:S(2)}) collective-permute-start(f32[160,128]{1,0:T(8,128)} %get-tuple-element.22), channel_id=1, source_target_pairs={{0,3},{1,0},{2,1},{3,2},{4,7},{5,4},{6,5},{7,6},{8,11},{9,8},{10,9... | collective-permute-start | bytes 245768 | tf_op jit(solution)/shard_map/ppermute | solution.py:23
  27.4 2.1 %collective-permute-done.10 = f32[160,128]{1,0:T(8,128)S(1)} collective-permute-done((f32[160,128]{1,0:T(8,128)}, f32[160,128]{1,0:T(8,128)S(1)}, u32[]{:S(2)}, u32[]{:S(2)}) %collective-permute-start.10) | collective-permute-done | bytes 81952 | tf_op jit(solution)/shard_map/ppermute | solution.py:23
  29.5 4.0 %collective-permute-done.8 = f32[160,128]{1,0:T(8,128)S(1)} collective-permute-done((f32[160,128]{1,0:T(8,128)}, f32[160,128]{1,0:T(8,128)S(1)}, u32[]{:S(2)}, u32[]{:S(2)}) %collective-permute-start.8) | collective-permute-done | bytes 81952 | tf_op jit(solution)/shard_map/ppermute | solution.py:23
  33.6 1.7 %collective-permute-done.9 = f32[160,128]{1,0:T(8,128)S(1)} collective-permute-done((f32[160,128]{1,0:T(8,128)}, f32[160,128]{1,0:T(8,128)S(1)}, u32[]{:S(2)}, u32[]{:S(2)}) %collective-permute-start.9) | collective-permute-done | bytes 81952 | tf_op jit(solution)/shard_map/ppermute | solution.py:23
  36.2 1.8 %collective-permute-start.13 = (f32[160,128]{1,0:T(8,128)S(1)}, f32[160,128]{1,0:T(8,128)S(1)}, u32[]{:S(2)}, u32[]{:S(2)}) collective-permute-start(f32[160,128]{1,0:T(8,128)S(1)} %add_add_fusion.1), channel_id=1, source_target_pairs={{0,24},{8,0},{16,8},{24,16},{1,25},{9,1},{17,9},{25,17},{2,26},{10... | collective-permute-start | bytes 245768 | tf_op jit(solution)/shard_map/ppermute | solution.py:23
  38.2 1.5 %collective-permute-start.12 = (f32[160,128]{1,0:T(8,128)S(1)}, f32[160,128]{1,0:T(8,128)S(1)}, u32[]{:S(2)}, u32[]{:S(2)}) collective-permute-start(f32[160,128]{1,0:T(8,128)S(1)} %add_add_fusion.1), channel_id=1, source_target_pairs={{0,16},{8,24},{16,0},{24,8},{1,17},{9,25},{17,1},{25,9},{2,18},{10... | collective-permute-start | bytes 245768 | tf_op jit(solution)/shard_map/ppermute | solution.py:23
  40.9 1.7 %collective-permute-start.1 = (f32[128,1024]{1,0:T(8,128)S(1)}, f32[128,1024]{1,0:T(8,128)S(1)}, u32[]{:S(2)}, u32[]{:S(2)}) collective-permute-start(f32[128,1024]{1,0:T(8,128)S(1)} %get-tuple-element.24), channel_id=1, source_target_pairs={{0,8},{8,16},{16,24},{24,0},{1,9},{9,17},{17,25},{25,1},{2,10},{10... | collective-permute-start | bytes 1572872 | tf_op jit(solution)/shard_map/ppermute | solution.py:23
  42.6 1.5 %collective-permute-start.2 = (f32[128,1024]{1,0:T(8,128)S(1)}, f32[128,1024]{1,0:T(8,128)S(1)}, u32[]{:S(2)}, u32[]{:S(2)}) collective-permute-start(f32[128,1024]{1,0:T(8,128)S(1)} %get-tuple-element.26), channel_id=1, source_target_pairs={{0,16},{8,24},{16,0},{24,8},{1,17},{9,25},{17,1},{25,9},{2,18},{10... | collective-permute-start | bytes 1572872 | tf_op jit(solution)/shard_map/ppermute | solution.py:23
  44.4 7.7 %collective-permute-done.12 = f32[160,128]{1,0:T(8,128)S(1)} collective-permute-done((f32[160,128]{1,0:T(8,128)S(1)}, f32[160,128]{1,0:T(8,128)S(1)}, u32[]{:S(2)}, u32[]{:S(2)}) %collective-permute-start.12) | collective-permute-done | bytes 81952 | tf_op jit(solution)/shard_map/ppermute | solution.py:23
  53.5 3.2 %collective-permute-start.15 = (f32[160,128]{1,0:T(8,128)S(1)}, f32[160,128]{1,0:T(8,128)S(1)}, u32[]{:S(2)}, u32[]{:S(2)}) collective-permute-start(f32[160,128]{1,0:T(8,128)S(1)} %add_add_fusion.refs_0_), channel_id=1, source_target_pairs={{0,2},{1,3},{2,0},{3,1},{4,6},{5,7},{6,4},{7,5},{8,10},{9,11},{10,... | collective-permute-start | bytes 245768 | tf_op jit(solution)/shard_map/ppermute | solution.py:23
  56.7 1.9 %collective-permute-done.14.refs_1_ = f32[160,128]{1,0:T(8,128)S(1)} collective-permute-done((f32[160,128]{1,0:T(8,128)S(1)}, f32[160,128]{1,0:T(8,128)S(1)}, u32[]{:S(2)}, u32[]{:S(2)}) %collective-permute-start.14) | collective-permute-done | bytes 81952 | tf_op jit(solution)/shard_map/ppermute | solution.py:23
  58.6 2.0 %collective-permute-start.16 = (f32[160,128]{1,0:T(8,128)S(1)}, f32[160,128]{1,0:T(8,128)S(1)}, u32[]{:S(2)}, u32[]{:S(2)}) collective-permute-start(f32[160,128]{1,0:T(8,128)S(1)} %add_add_fusion.refs_0_), channel_id=1, source_target_pairs={{0,3},{1,0},{2,1},{3,2},{4,7},{5,4},{6,5},{7,6},{8,11},{9,8},{10,9... | collective-permute-start | bytes 245768 | tf_op jit(solution)/shard_map/ppermute | solution.py:23
  60.6 2.4 %collective-permute-done.16.refs_3_ = f32[160,128]{1,0:T(8,128)S(1)} collective-permute-done((f32[160,128]{1,0:T(8,128)S(1)}, f32[160,128]{1,0:T(8,128)S(1)}, u32[]{:S(2)}, u32[]{:S(2)}) %collective-permute-start.16) | collective-permute-done | bytes 81952 | tf_op jit(solution)/shard_map/ppermute | solution.py:23
  63.7 1.8 %shard_map.40.refs_0_ = f32[640,128]{1,0:T(8,128)} custom-call(s32[3]{0:T(128)} %pad_add_fusion.where, f32[160,128]{1,0:T(8,128)} %copy-done.1, f32[160,128]{1,0:T(8,128)} %copy-done.6, f32[160,128]{1,0:T(8,128)} %copy-done.7, f32[160,128]{1,0:T(8,128)} %copy-done.8), custom_call_target="tpu_custom_call" | custom-call | bytes 655372 | tf_op jit(solution)/shard_map/pallas_call | solution.py:28
  66.5 3.4 %shard_map.37 = (bf16[512,1024]{1,0:T(8,128)(2,1)}, f32[512,512]{1,0:T(8,128)}, bf16[256,512]{1,0:T(8,128)(2,1)}) custom-call(s32[3]{0:T(128)} %pad_add_fusion.where, f32[128,1024]{1,0:T(8,128)} %get-tuple-element.25.own, f32[128,1024]{1,0:T(8,128)} %copy-done.10, f32[128,1024]{1,0:T(8,128)} %copy-done.11, f32[128,1024]{1,0:T(8,128)} %collective-permute-done.3.refs_2_), custom_call_target="tpu_custom_call" | custom-call | flops 805306368 | bytes 4456460 | tf_op jit(solution)/shard_map/pallas_call | solution.py:28
  70.6 7.8 %shard_map.41 = f32[256,1024]{1,0:T(8,128)} custom-call(s32[3]{0:T(128)} %pad_add_fusion.where, bf16[512,1024]{1,0:T(8,128)(2,1)} %get-tuple-element.14.normed, f32[512,512]{1,0:T(8,128)} %get-tuple-element.15.gram, bf16[256,512]{1,0:T(8,128)(2,1)} %get-tuple-element.16.columns, f32[640,128]{1,0:T(8,128)} %shard_map.40.refs_0_, f32[640,128]{1,0:T(8,128)} %copy-done.12), custom_call_target="tpu_custom_call" | custom-call | flops 3087007744 | bytes 4063244 | tf_op jit(solution)/shard_map/pallas_call | solution.py:28
  78.4 18.6 %all_to_all.5 = f32[4,64,1024]{2,1,0:T(8,128)S(1)} all-to-all(f32[4,64,1024]{2,1,0:T(8,128)} %bitcast.8), channel_id=1, replica_groups=mesh['dp'=4,'tensor'=2,'precond'=4] {'dp'}, dimensions={0} | all-to-all | bytes 2097152 | tf_op jit(solution)/shard_map/all_to_all | solution.py:250
  (53 shorter events, 13.9 us)
Async XLA Ops:
  0.0 18.4 %copy-start = (bf16[128,4096]{1,0:T(8,128)(2,1)S(1)}, bf16[128,4096]{1,0:T(8,128)(2,1)}, u32[]{:S(2)}) copy-start(bf16[128,4096]{1,0:T(8,128)(2,1)} %param.3) | copy-start | bytes 3145732
  1.8 17.4 %copy-start.9 = (bf16[4096]{0:T(1024)(128)(2,1)S(1)}, bf16[4096]{0:T(1024)(128)(2,1)}, u32[]{:S(2)}) copy-start(bf16[4096]{0:T(1024)(128)(2,1)} %param.4) | copy-start | bytes 24580
  1.8 9.7 %collective-permute-start.4 = (f32[128,384]{1,0:T(8,128)S(1)}, f32[128,384]{1,0:T(8,128)S(1)}, u32[]{:S(2)}, u32[]{:S(2)}) collective-permute-start(f32[128,384]{1,0:T(8,128)S(1)} %get-tuple-element.28), channel_id=1, source_target_pairs={{0,8},{8,16},{16,24},{24,0},{1,9},{9,17},{17,25},{25,1},{2,10},{10... | collective-permute-start | bytes 589832 | tf_op jit(solution)/shard_map/ppermute | solution.py:23
  4.8 10.1 %collective-permute-start.5 = (f32[128,384]{1,0:T(8,128)S(1)}, f32[128,384]{1,0:T(8,128)S(1)}, u32[]{:S(2)}, u32[]{:S(2)}) collective-permute-start(f32[128,384]{1,0:T(8,128)S(1)} %get-tuple-element.30), channel_id=1, source_target_pairs={{0,16},{8,24},{16,0},{24,8},{1,17},{9,25},{17,1},{25,9},{2,18},{10... | collective-permute-start | bytes 589832 | tf_op jit(solution)/shard_map/ppermute | solution.py:23
  6.3 8.8 %collective-permute-start.6 = (f32[128,384]{1,0:T(8,128)S(1)}, f32[128,384]{1,0:T(8,128)S(1)}, u32[]{:S(2)}, u32[]{:S(2)}) collective-permute-start(f32[128,384]{1,0:T(8,128)S(1)} %get-tuple-element.27), channel_id=1, source_target_pairs={{0,24},{8,0},{16,8},{24,16},{1,25},{9,1},{17,9},{25,17},{2,26},{10... | collective-permute-start | bytes 589832 | tf_op jit(solution)/shard_map/ppermute | solution.py:23
  11.5 3.6 %copy-start.3 = (f32[128,384]{1,0:T(8,128)}, f32[128,384]{1,0:T(8,128)S(1)}, u32[]{:S(2)}) copy-start(f32[128,384]{1,0:T(8,128)S(1)} %collective-permute-done.4.refs_0_) | copy-start | bytes 589828
  18.4 1.8 %collective-permute-start.7 = (f32[640,128]{1,0:T(8,128)}, f32[640,128]{1,0:T(8,128)S(1)}, u32[]{:S(2)}, u32[]{:S(2)}) collective-permute-start(f32[640,128]{1,0:T(8,128)} %get-tuple-element.18), channel_id=1, source_target_pairs={{0,4},{4,0},{1,5},{5,1},{2,6},{6,2},{3,7},{7,3},{8,12},{12,8},{9,1... | collective-permute-start | bytes 983048 | tf_op jit(solution)/shard_map/ppermute | solution.py:23
  18.7 8.7 %collective-permute-start = (f32[1,128]{1,0:T(1,128)S(1)}, f32[1,128]{1,0:T(1,128)S(1)}, u32[]{:S(2)}, u32[]{:S(2)}) collective-permute-start(f32[1,128]{1,0:T(1,128)S(1)} %bitcast.9), channel_id=1, source_target_pairs={{0,4},{4,0},{1,5},{5,1},{2,6},{6,2},{3,7},{7,3},{8,12},{12,8},{9,1... | collective-permute-start | bytes 1544 | tf_op jit(solution)/shard_map/ppermute | solution.py:23
  22.8 6.7 %collective-permute-start.10 = (f32[160,128]{1,0:T(8,128)}, f32[160,128]{1,0:T(8,128)S(1)}, u32[]{:S(2)}, u32[]{:S(2)}) collective-permute-start(f32[160,128]{1,0:T(8,128)} %get-tuple-element.22), channel_id=1, source_target_pairs={{0,3},{1,0},{2,1},{3,2},{4,7},{5,4},{6,5},{7,6},{8,11},{9,8},{10,9... | collective-permute-start | bytes 245768 | tf_op jit(solution)/shard_map/ppermute | solution.py:23
  26.4 7.2 %collective-permute-start.8 = (f32[160,128]{1,0:T(8,128)}, f32[160,128]{1,0:T(8,128)S(1)}, u32[]{:S(2)}, u32[]{:S(2)}) collective-permute-start(f32[160,128]{1,0:T(8,128)} %get-tuple-element.20), channel_id=1, source_target_pairs={{0,1},{1,2},{2,3},{3,0},{4,5},{5,6},{6,7},{7,4},{8,9},{9,10},{10,1... | collective-permute-start | bytes 245768 | tf_op jit(solution)/shard_map/ppermute | solution.py:23
  26.4 8.8 %collective-permute-start.9 = (f32[160,128]{1,0:T(8,128)}, f32[160,128]{1,0:T(8,128)S(1)}, u32[]{:S(2)}, u32[]{:S(2)}) collective-permute-start(f32[160,128]{1,0:T(8,128)} %get-tuple-element.21), channel_id=1, source_target_pairs={{0,2},{1,3},{2,0},{3,1},{4,6},{5,7},{6,4},{7,5},{8,10},{9,11},{10,... | collective-permute-start | bytes 245768 | tf_op jit(solution)/shard_map/ppermute | solution.py:23
  36.2 8.0 %collective-permute-start.13 = (f32[160,128]{1,0:T(8,128)S(1)}, f32[160,128]{1,0:T(8,128)S(1)}, u32[]{:S(2)}, u32[]{:S(2)}) collective-permute-start(f32[160,128]{1,0:T(8,128)S(1)} %add_add_fusion.1), channel_id=1, source_target_pairs={{0,24},{8,0},{16,8},{24,16},{1,25},{9,1},{17,9},{25,17},{2,26},{10... | collective-permute-start | bytes 245768 | tf_op jit(solution)/shard_map/ppermute | solution.py:23
  37.9 6.4 %collective-permute-start.11 = (f32[160,128]{1,0:T(8,128)S(1)}, f32[160,128]{1,0:T(8,128)S(1)}, u32[]{:S(2)}, u32[]{:S(2)}) collective-permute-start(f32[160,128]{1,0:T(8,128)S(1)} %add_add_fusion.1), channel_id=1, source_target_pairs={{0,8},{8,16},{16,24},{24,0},{1,9},{9,17},{17,25},{25,1},{2,10},{10... | collective-permute-start | bytes 245768 | tf_op jit(solution)/shard_map/ppermute | solution.py:23
  38.2 13.9 %collective-permute-start.12 = (f32[160,128]{1,0:T(8,128)S(1)}, f32[160,128]{1,0:T(8,128)S(1)}, u32[]{:S(2)}, u32[]{:S(2)}) collective-permute-start(f32[160,128]{1,0:T(8,128)S(1)} %add_add_fusion.1), channel_id=1, source_target_pairs={{0,16},{8,24},{16,0},{24,8},{1,17},{9,25},{17,1},{25,9},{2,18},{10... | collective-permute-start | bytes 245768 | tf_op jit(solution)/shard_map/ppermute | solution.py:23
  40.9 24.6 %collective-permute-start.1 = (f32[128,1024]{1,0:T(8,128)S(1)}, f32[128,1024]{1,0:T(8,128)S(1)}, u32[]{:S(2)}, u32[]{:S(2)}) collective-permute-start(f32[128,1024]{1,0:T(8,128)S(1)} %get-tuple-element.24), channel_id=1, source_target_pairs={{0,8},{8,16},{16,24},{24,0},{1,9},{9,17},{17,25},{25,1},{2,10},{10... | collective-permute-start | bytes 1572872 | tf_op jit(solution)/shard_map/ppermute | solution.py:23
  42.6 22.9 %collective-permute-start.2 = (f32[128,1024]{1,0:T(8,128)S(1)}, f32[128,1024]{1,0:T(8,128)S(1)}, u32[]{:S(2)}, u32[]{:S(2)}) collective-permute-start(f32[128,1024]{1,0:T(8,128)S(1)} %get-tuple-element.26), channel_id=1, source_target_pairs={{0,16},{8,24},{16,0},{24,8},{1,17},{9,25},{17,1},{25,9},{2,18},{10... | collective-permute-start | bytes 1572872 | tf_op jit(solution)/shard_map/ppermute | solution.py:23
  44.1 21.4 %collective-permute-start.3 = (f32[128,1024]{1,0:T(8,128)S(1)}, f32[128,1024]{1,0:T(8,128)}, u32[]{:S(2)}, u32[]{:S(2)}) collective-permute-start(f32[128,1024]{1,0:T(8,128)S(1)} %get-tuple-element.23), channel_id=1, source_target_pairs={{0,24},{8,0},{16,8},{24,16},{1,25},{9,1},{17,9},{25,17},{2,26},{10... | collective-permute-start | bytes 1572872 | tf_op jit(solution)/shard_map/ppermute | solution.py:23
  52.1 10.9 %copy-start.1 = (f32[160,128]{1,0:T(8,128)}, f32[160,128]{1,0:T(8,128)S(1)}, u32[]{:S(2)}) copy-start(f32[160,128]{1,0:T(8,128)S(1)} %add_add_fusion.refs_0_) | copy-start | bytes 245764
  52.1 6.5 %collective-permute-start.14 = (f32[160,128]{1,0:T(8,128)S(1)}, f32[160,128]{1,0:T(8,128)S(1)}, u32[]{:S(2)}, u32[]{:S(2)}) collective-permute-start(f32[160,128]{1,0:T(8,128)S(1)} %add_add_fusion.refs_0_), channel_id=1, source_target_pairs={{0,1},{1,2},{2,3},{3,0},{4,5},{5,6},{6,7},{7,4},{8,9},{9,10},{10,1... | collective-permute-start | bytes 245768 | tf_op jit(solution)/shard_map/ppermute | solution.py:23
  53.5 7.1 %collective-permute-start.15 = (f32[160,128]{1,0:T(8,128)S(1)}, f32[160,128]{1,0:T(8,128)S(1)}, u32[]{:S(2)}, u32[]{:S(2)}) collective-permute-start(f32[160,128]{1,0:T(8,128)S(1)} %add_add_fusion.refs_0_), channel_id=1, source_target_pairs={{0,2},{1,3},{2,0},{3,1},{4,6},{5,7},{6,4},{7,5},{8,10},{9,11},{10,... | collective-permute-start | bytes 245768 | tf_op jit(solution)/shard_map/ppermute | solution.py:23
  58.6 4.4 %copy-start.6 = (f32[160,128]{1,0:T(8,128)}, f32[160,128]{1,0:T(8,128)S(1)}, u32[]{:S(2)}) copy-start(f32[160,128]{1,0:T(8,128)S(1)} %collective-permute-done.14.refs_1_) | copy-start | bytes 245764
  58.6 4.4 %collective-permute-start.16 = (f32[160,128]{1,0:T(8,128)S(1)}, f32[160,128]{1,0:T(8,128)S(1)}, u32[]{:S(2)}, u32[]{:S(2)}) collective-permute-start(f32[160,128]{1,0:T(8,128)S(1)} %add_add_fusion.refs_0_), channel_id=1, source_target_pairs={{0,3},{1,0},{2,1},{3,2},{4,7},{5,4},{6,5},{7,6},{8,11},{9,8},{10,9... | collective-permute-start | bytes 245768 | tf_op jit(solution)/shard_map/ppermute | solution.py:23
  60.6 2.5 %copy-start.7 = (f32[160,128]{1,0:T(8,128)}, f32[160,128]{1,0:T(8,128)S(1)}, u32[]{:S(2)}) copy-start(f32[160,128]{1,0:T(8,128)S(1)} %collective-permute-done.15.refs_2_) | copy-start | bytes 245764
  65.4 4.4 %collective-permute-start.17 = (f32[640,128]{1,0:T(8,128)}, f32[640,128]{1,0:T(8,128)S(1)}, u32[]{:S(2)}, u32[]{:S(2)}) collective-permute-start(f32[640,128]{1,0:T(8,128)} %shard_map.40.refs_0_), channel_id=1, source_target_pairs={{0,4},{4,0},{1,5},{5,1},{2,6},{6,2},{3,7},{7,3},{8,12},{12,8},{9,1... | collective-permute-start | bytes 983048 | tf_op jit(solution)/shard_map/ppermute | solution.py:23
  (7 other events, 5.2 us)

commit v2 on v1

v2 whole, which is shorter than its diff:
```python
import functools

import jax
import jax.numpy as jnp
from jax import lax
from jax.experimental import pallas as pl
from jax.experimental.pallas import tpu as pltpu
from jax.sharding import PartitionSpec as P

BLK = 1024

epsilon = 1e-06
damping = 0.01

f32 = jnp.float32
bf16 = jnp.bfloat16
VMEM = pl.BlockSpec(memory_space=pltpu.VMEM)
SMEM = pl.BlockSpec(memory_space=pltpu.SMEM)


def swap(value, axis, by):
    size = lax.axis_size(axis)
    return lax.ppermute(value, axis, [(i, i ^ by) for i in range(size)])


def call(kernel, outs, *operands, scratch=(), flops=0):
    moved = sum(a.size * a.dtype.itemsize for a in (*operands, *outs))
    return pl.pallas_call(
        kernel,
        out_shape=list(outs),
        in_specs=[SMEM] + [VMEM] * (len(operands) - 1),
        out_specs=[VMEM] * len(outs),
        scratch_shapes=list(scratch),
        compiler_params=pltpu.CompilerParams(vmem_limit_bytes=24 * 2**20),
        cost_estimate=pl.CostEstimate(flops=flops, bytes_accessed=moved, transcendentals=0),
    )(*operands)


def nt(left, right):
    return lax.dot_general(left, right, (((1,), (1,)), ((), ())), preferred_element_type=f32)


def nn(left, right):
    return lax.dot_general(left, right, (((1,), (0,)), ((), ())), preferred_element_type=f32)


def halves(value):
    high = value.astype(bf16)
    return high, (value - high.astype(f32)).astype(bf16)


def product(left, right):
    return nn(left[0], right[0]) + (nn(left[0], right[1]) + nn(left[1], right[0]))


def rows_at(index, count):
    return pl.ds(pl.multiple_of(index * count, 8), count)


def gram_kernel(nten, npre, where, own, *refs):
    received, outs, whole, packed = refs[: -nten - 2], refs[-nten - 2 : -2], refs[-2], refs[-1]
    me, ten, pre = where[0], where[1], where[2]
    size, dp = own.shape[0], len(received) + 1
    whole[rows_at(me, size)] = own[...].astype(bf16)
    for by, piece in enumerate(received, 1):
        whole[rows_at(me ^ by, size)] = piece[...].astype(bf16)
    at = 0
    for i in range(dp):
        rows = nt(whole[i * size : (i + 1) * size], whole[i * size :])
        for j in range(dp - i):
            packed[at * size : (at + 1) * size] = rows[:, j * size : (j + 1) * size]
            at += 1
    if at * size < packed.shape[0]:
        packed[at * size :] = jnp.zeros((packed.shape[0] - at * size, size), f32)
    count = packed.shape[0] // (nten * npre)
    for to, out in enumerate(outs):
        for by in range(npre):
            out[by * count : (by + 1) * count] = packed[rows_at((ten ^ to) * npre + (pre ^ by), count)]


def output_rows(dp, nb, npre, me, pre, count, width):
    each, share = width // (dp * npre), dp // nb
    made = lax.broadcasted_iota(jnp.int32, (count, width), 0)
    column = lax.broadcasted_iota(jnp.int32, (count, width), 1)
    target = lax.rem(me, share) * nb + ((me // share) ^ (made // each))
    return ((target * npre + pre) * each + lax.rem(made, each) == column).astype(f32)


def normed_kernel(nb, npre, where, own, *refs):
    received, (normed, high, low, columns) = refs[:-4], refs[-4:]
    me, pre = where[0], where[2]
    size, dp = own.shape[0], len(received) + 1
    normed[rows_at(me, size)] = own[...].astype(bf16)
    for by, piece in enumerate(received, 1):
        normed[rows_at(me ^ by, size)] = piece[...].astype(bf16)
    high[...], low[...] = halves(nt(normed[...], normed[...]))
    select = output_rows(dp, nb, npre, me, pre, columns.shape[0], normed.shape[1])
    columns[...] = nt(select.astype(bf16), normed[...]).astype(bf16)


def root_kernel(dp, nb, npre, nten, where, normed, high, low, columns, *refs):
    pieces, outs, packed, inner = refs[: nten * npre], refs[nten * npre : -2], refs[-2], refs[-1]
    me, ten, pre = where[0], where[1], where[2]
    for at, piece in enumerate(pieces):
        packed[rows_at((ten ^ at // npre) * npre + (pre ^ at % npre), piece.shape[0])] = piece[...]
    total, width = normed.shape
    size, at = total // dp, 0
    for i in range(dp):
        for j in range(i, dp):
            tile = packed[at * size : (at + 1) * size]
            inner[i * size : (i + 1) * size, j * size : (j + 1) * size] = tile
            if j > i:
                inner[j * size : (j + 1) * size, i * size : (i + 1) * size] = tile.T
            at += 1
    tokens_gram = high[...], low[...]
    both = inner[...] * (tokens_gram[0].astype(f32) + tokens_gram[1].astype(f32))
    power = jnp.sum(jnp.sum(both, axis=0, keepdims=True), axis=1, keepdims=True)
    scaling = 2.0 * (power / (float(total) * float(total)) / width + damping)
    damp = damping / scaling
    base = (5.0 - damp) / 4.0
    core = halves(inner[...] * (1.0 / (scaling * (float(total) * float(total)))))
    mixed = halves(product(tokens_gram, core))
    rows = nn(columns[...], core[0]) + nn(columns[...], core[1])

    def step(value, weight):
        return base * value - 0.25 * product(halves(value), mixed) + weight * rows

    weight = 0.25 * damp
    value = step(-rows, weight)
    for _ in range(3):
        weight = weight * base
        value = step(value, weight)
    weight = weight * base
    value = step(value, weight - 1.25)
    root = lax.rsqrt(jnp.sqrt(scaling))
    value = halves(value * (0.25 * root))
    alone = (5.0 * base - damp * base * base * base * base * base) * 0.25 * root
    made = nn(value[0], normed[...]) + nn(value[1], normed[...])
    made = made + alone * output_rows(dp, nb, npre, me, pre, made.shape[0], width)
    each = outs[0].shape[0]
    for by, out in enumerate(outs):
        out[...] = made[by * each : (by + 1) * each]


def program(tokens, gain, cotangent):
    dp, nten, npre = (lax.axis_size(name) for name in ("dp", "tensor", "precond"))
    me, ten, pre = (lax.axis_index(name) for name in ("dp", "tensor", "precond"))
    where = jnp.stack([me, ten, pre]).astype(jnp.int32)
    size, width = tokens.shape
    total = size * dp
    nb = width // BLK
    share = dp // nb
    assert nb * BLK == width and share * nb == dp
    assert all(n & (n - 1) == 0 for n in (dp, nten, npre))
    hidden = cotangent.shape[1] // (nten * dp)
    assert hidden * nten * dp == cotangent.shape[1]

    def cotangent_part(to):
        return lax.dynamic_slice_in_dim(cotangent, (ten * dp + to) * hidden, hidden, 1)

    cotangents = [swap(cotangent_part(me ^ by).astype(f32), "dp", by) for by in range(1, dp)]
    cotangents = [cotangent_part(me)] + cotangents

    values = tokens.astype(f32)
    square = jnp.sum(values * values, axis=1)[None, :]
    square = square + sum(swap(square, "tensor", by) for by in range(1, nten))
    inverse = lax.rsqrt(square[0][:, None] / (width * nten) + epsilon)

    def normed_part(to):
        at = (to // share) * BLK
        part = lax.dynamic_slice_in_dim(tokens, at, BLK, 1).astype(f32)
        scale = lax.dynamic_slice_in_dim(gain, at, BLK, 0).astype(f32)
        return part * inverse * scale

    normed_parts = [swap(normed_part(me ^ by), "dp", by) for by in range(1, dp)]
    normed_parts = [normed_part(me)] + normed_parts

    tiles = dp * (dp + 1) // 2
    piece = -(-tiles * size // (nten * npre * 8)) * 8
    packed = pltpu.VMEM((nten * npre * piece, size), f32)
    part = jax.ShapeDtypeStruct((npre * piece, size), f32)
    parts = call(
        functools.partial(gram_kernel, nten, npre),
        [part] * nten,
        where,
        *cotangents,
        scratch=[pltpu.VMEM((total, hidden), bf16), packed],
        flops=tiles * size * size * hidden * 2,
    )
    part = parts[0] + sum(swap(parts[to], "tensor", to) for to in range(1, nten))
    summed = part[:piece] + sum(
        swap(part[by * piece : (by + 1) * piece], "precond", by) for by in range(1, npre)
    )
    summed = summed + sum(swap(summed, "dp", by) for by in range(1, dp))
    pieces = [summed] + [swap(summed, "precond", by) for by in range(1, npre)]
    pieces = pieces + [swap(one, "tensor", to) for to in range(1, nten) for one in pieces]

    each = BLK // (dp * npre)
    made = nb * each
    normed, high, low, columns = call(
        functools.partial(normed_kernel, nb, npre),
        [
            jax.ShapeDtypeStruct((total, BLK), bf16),
            jax.ShapeDtypeStruct((total, total), bf16),
            jax.ShapeDtypeStruct((total, total), bf16),
            jax.ShapeDtypeStruct((made, total), bf16),
        ],
        where,
        *normed_parts,
        flops=2 * total * total * BLK + 2 * made * BLK * total,
    )
    rows = call(
        functools.partial(root_kernel, dp, nb, npre, nten),
        [jax.ShapeDtypeStruct((each, BLK), f32)] * nb,
        where,
        normed,
        high,
        low,
        columns,
        *pieces,
        scratch=[packed, pltpu.VMEM((total, total), f32)],
        flops=2 * total * total * (3 * total + 17 * made),
    )
    result = jnp.zeros((nb, each, BLK), f32)
    for by in range(nb):
        pairs = [(b * share + m, m * nb + (b ^ by)) for b in range(nb) for m in range(share)]
        sent = rows[by]
        if any(a != b for a, b in pairs):
            sent = lax.ppermute(sent, "dp", pairs)
        result = lax.dynamic_update_slice_in_dim(result, sent[None], lax.rem(me, nb) ^ by, 0)
    return result


def solution(mesh):
    in_specs = (P("dp", "tensor"), P("tensor"), P("dp", "precond"))
    out_specs = P("tensor", ("dp", "precond"), None)
    return jax.shard_map(program, mesh=mesh, in_specs=in_specs, out_specs=out_specs, check_vma=False)
```

time: 98.3 us -> 88 us (0.90)
  waiting for transfers between devices: 27.7 us -> 51.9 us
  blocking collectives: 18.6 us -> 0 us
  Pallas kernels: 17.3 us -> 2.77 us
  other arithmetic: 4.79 us -> 1.91 us
  local copies, waits for them, and re-layouts: 4.72 us -> 6.35 us
    ppermute x18 -> x24, waiting for transfers between devices: 27.7 us -> 51.9 us  [the longest x21 40.2 us: swap(): return lax.ppermute(value, axis, [(i, i ^ by) for i in range(size)])]
    all_to_all x1 -> x0, blocking collectives: 18.6 us -> none  [body(): return lax.all_to_all(rows, 'dp', 0, 0, tiled=True)]
    pallas_call x5 -> x2, Pallas kernels: 17.3 us -> 2.77 us  [call(): pl.pallas_call(kernel, out_shape=list(outs), in_specs=[SMEM] + [VMEM] * (...]
    pallas_call x0 -> x1, local copies, waits for them, and re-layouts: none -> 5.45 us  [call(): pl.pallas_call(kernel, out_shape=list(outs), in_specs=[SMEM] + [VMEM] * (...]
    unnamed x27 -> x6, local copies, waits for them, and re-layouts: 4.72 us -> 0.02 us
    ppermute x18 -> x24, starting transfers between devices: 24.7 us -> 24.7 us  [the longest x21 21.1 us: swap(): return lax.ppermute(value, axis, [(i, i ^ by) for i in range(size)])]
  transfers between devices with their start and end apart: 18 -> 24, of which waited for: 10 -> 14; matrix products, arithmetic and copies ran while one was open for 2% -> 1% of each run, Pallas kernels for 7% -> 3%
where the time goes in v2:
time: 88 us; the launch traced here: 87.9 us
  waiting for transfers between devices  51.9 us (59%)
  starting transfers between devices  24.7 us (28%)
  local copies, waits for them, and re-layouts  6.35 us (7%)
  Pallas kernels  2.77 us (3%)
  other arithmetic  1.91 us (2%)
    ppermute x21, waiting for transfers between devices, swap(): return lax.ppermute(value, axis, [(i, i ^ by) for i in range(size)])  40.2 us
    ppermute x21, starting transfers between devices, swap(): return lax.ppermute(value, axis, [(i, i ^ by) for i in range(size)])  21.1 us
    ppermute x3, waiting for transfers between devices, program(): sent = lax.ppermute(sent, 'dp', pairs)  11.7 us
    pallas_call x1, local copies, waits for them, and re-layouts, call(): pl.pallas_call(kernel, out_shape=list(outs), in_specs=[SMEM] + [VMEM] * (...  5.45 us
    ppermute x3, starting transfers between devices, program(): sent = lax.ppermute(sent, 'dp', pairs)  3.55 us
    pallas_call x2, Pallas kernels, call(): pl.pallas_call(kernel, out_shape=list(outs), in_specs=[SMEM] + [VMEM] * (...  2.77 us
  transfers between devices with their start and end apart: 24, of which 14 were waited for; matrix products, arithmetic and copies ran while one was open for 1% of the time, Pallas kernels for 3%

profile of v2, /device:TPU:0, one launch (start us, length us, event | category | flops | bytes accessed | tf_op | source)
XLA Modules:
  0.0 87.9 jit_solution(6101503287692464862)
XLA Ops:
  0.0 1.2 %dynamic-slice_convert_fusion = (f32[128,384]{1,0:T(8,128)S(1)}, f32[128,384]{1,0:T(8,128)S(1)}, bf16[128,384]{1,0:T(8,128)(2,1)S(1)}, f32[128,384]{1,0:T(8,128)S(1)}) fusion(bf16[128,3072]{1,0:T(8,128)(2,1)} %param.5, s32[]{:T(128)S(6)} %select_n.53, s32[]{:T(128)S(6)} %select_n.51, s32[]{:T(128)S(6)} %select_n.50, s32[]{:T(128)S(6)} %select_n.52), kind=kLoop, calls=%fused_computation.9 | loop fusion | flops 147456 | bytes 1081360 | tf_op jit(solution)/shard_map/convert_element_type | solution.py:161
  1.2 3.0 %collective-permute-start.4 = (f32[128,384]{1,0:T(8,128)S(1)}, f32[128,384]{1,0:T(8,128)S(1)}, u32[]{:S(2)}, u32[]{:S(2)}) collective-permute-start(f32[128,384]{1,0:T(8,128)S(1)} %get-tuple-element.38), channel_id=1, source_target_pairs={{0,8},{8,0},{16,24},{24,16},{1,9},{9,1},{17,25},{25,17},{2,10},{10... | collective-permute-start | bytes 589832 | tf_op jit(solution)/shard_map/ppermute | solution.py:23
  4.2 1.5 %collective-permute-start.5 = (f32[128,384]{1,0:T(8,128)S(1)}, f32[128,384]{1,0:T(8,128)S(1)}, u32[]{:S(2)}, u32[]{:S(2)}) collective-permute-start(f32[128,384]{1,0:T(8,128)S(1)} %get-tuple-element.40), channel_id=1, source_target_pairs={{0,16},{8,24},{16,0},{24,8},{1,17},{9,25},{17,1},{25,9},{2,18},{10... | collective-permute-start | bytes 589832 | tf_op jit(solution)/shard_map/ppermute | solution.py:23
  6.2 3.7 %collective-permute-done.4.refs_0_ = f32[128,384]{1,0:T(8,128)S(1)} collective-permute-done((f32[128,384]{1,0:T(8,128)S(1)}, f32[128,384]{1,0:T(8,128)S(1)}, u32[]{:S(2)}, u32[]{:S(2)}) %collective-permute-start.4) | collective-permute-done | bytes 196640 | tf_op jit(solution)/shard_map/ppermute | solution.py:23
  10.0 4.8 %collective-permute-done.5.refs_1_ = f32[128,384]{1,0:T(8,128)S(1)} collective-permute-done((f32[128,384]{1,0:T(8,128)S(1)}, f32[128,384]{1,0:T(8,128)S(1)}, u32[]{:S(2)}, u32[]{:S(2)}) %collective-permute-start.5) | collective-permute-done | bytes 196640 | tf_op jit(solution)/shard_map/ppermute | solution.py:23
  16.0 1.6 %collective-permute-done.7 = f32[640,128]{1,0:T(8,128)S(1)} collective-permute-done((f32[640,128]{1,0:T(8,128)S(1)}, f32[640,128]{1,0:T(8,128)S(1)}, u32[]{:S(2)}, u32[]{:S(2)}) %collective-permute-start.7) | collective-permute-done | bytes 327712 | tf_op jit(solution)/shard_map/ppermute | solution.py:23
  17.6 3.7 %collective-permute-start.10 = (f32[160,128]{1,0:T(8,128)S(1)}, f32[160,128]{1,0:T(8,128)S(1)}, u32[]{:S(2)}, u32[]{:S(2)}) collective-permute-start(f32[160,128]{1,0:T(8,128)S(1)} %get-tuple-element.42), channel_id=1, source_target_pairs={{0,3},{1,2},{2,1},{3,0},{4,7},{5,6},{6,5},{7,4},{8,11},{9,10},{10,... | collective-permute-start | bytes 245768 | tf_op jit(solution)/shard_map/ppermute | solution.py:23
  22.4 1.3 %collective-permute-start.1 = (f32[128,1024]{1,0:T(8,128)S(1)}, f32[128,1024]{1,0:T(8,128)S(1)}, u32[]{:S(2)}, u32[]{:S(2)}) collective-permute-start(f32[128,1024]{1,0:T(8,128)S(1)} %get-tuple-element.34), channel_id=1, source_target_pairs={{0,8},{8,0},{16,24},{24,16},{1,9},{9,1},{17,25},{25,17},{2,10},{10... | collective-permute-start | bytes 1572872 | tf_op jit(solution)/shard_map/ppermute | solution.py:23
  24.9 1.5 %collective-permute-start.3 = (f32[128,1024]{1,0:T(8,128)S(1)}, f32[128,1024]{1,0:T(8,128)S(1)}, u32[]{:S(2)}, u32[]{:S(2)}) collective-permute-start(f32[128,1024]{1,0:T(8,128)S(1)} %get-tuple-element.33), channel_id=1, source_target_pairs={{0,24},{8,16},{16,8},{24,0},{1,25},{9,17},{17,9},{25,1},{2,26},{10... | collective-permute-start | bytes 1572872 | tf_op jit(solution)/shard_map/ppermute | solution.py:23
  28.5 1.3 %collective-permute-start.11 = (f32[160,128]{1,0:T(8,128)S(1)}, f32[160,128]{1,0:T(8,128)S(1)}, u32[]{:S(2)}, u32[]{:S(2)}) collective-permute-start(f32[160,128]{1,0:T(8,128)S(1)} %slice_add_fusion), channel_id=1, source_target_pairs={{0,8},{8,0},{16,24},{24,16},{1,9},{9,1},{17,25},{25,17},{2,10},{10... | collective-permute-start | bytes 245768 | tf_op jit(solution)/shard_map/ppermute | solution.py:23
  30.6 18.1 %collective-permute-done.11 = f32[160,128]{1,0:T(8,128)S(1)} collective-permute-done((f32[160,128]{1,0:T(8,128)S(1)}, f32[160,128]{1,0:T(8,128)S(1)}, u32[]{:S(2)}, u32[]{:S(2)}) %collective-permute-start.11) | collective-permute-done | bytes 81952 | tf_op jit(solution)/shard_map/ppermute | solution.py:23
  48.7 1.5 %collective-permute-start.13 = (f32[160,128]{1,0:T(8,128)S(1)}, f32[160,128]{1,0:T(8,128)S(1)}, u32[]{:S(2)}, u32[]{:S(2)}) collective-permute-start(f32[160,128]{1,0:T(8,128)S(1)} %slice_add_fusion), channel_id=1, source_target_pairs={{0,24},{8,16},{16,8},{24,0},{1,25},{9,17},{17,9},{25,1},{2,26},{10... | collective-permute-start | bytes 245768 | tf_op jit(solution)/shard_map/ppermute | solution.py:23
  50.2 3.8 %collective-permute-done.13 = f32[160,128]{1,0:T(8,128)S(1)} collective-permute-done((f32[160,128]{1,0:T(8,128)S(1)}, f32[160,128]{1,0:T(8,128)S(1)}, u32[]{:S(2)}, u32[]{:S(2)}) %collective-permute-start.13) | collective-permute-done | bytes 81952 | tf_op jit(solution)/shard_map/ppermute | solution.py:23
  54.1 1.5 %collective-permute-start.14 = (f32[160,128]{1,0:T(8,128)S(1)}, f32[160,128]{1,0:T(8,128)S(1)}, u32[]{:S(2)}, u32[]{:S(2)}) collective-permute-start(f32[160,128]{1,0:T(8,128)S(1)} %add_add_fusion), channel_id=1, source_target_pairs={{0,1},{1,0},{2,3},{3,2},{4,5},{5,4},{6,7},{7,6},{8,9},{9,8},{10,11... | collective-permute-start | bytes 245768 | tf_op jit(solution)/shard_map/ppermute | solution.py:23
  55.6 2.6 %collective-permute-start.15 = (f32[160,128]{1,0:T(8,128)S(1)}, f32[160,128]{1,0:T(8,128)S(1)}, u32[]{:S(2)}, u32[]{:S(2)}) collective-permute-start(f32[160,128]{1,0:T(8,128)S(1)} %add_add_fusion), channel_id=1, source_target_pairs={{0,2},{1,3},{2,0},{3,1},{4,6},{5,7},{6,4},{7,5},{8,10},{9,11},{10,... | collective-permute-start | bytes 245768 | tf_op jit(solution)/shard_map/ppermute | solution.py:23
  59.1 3.2 %collective-permute-done.15 = f32[160,128]{1,0:T(8,128)S(1)} collective-permute-done((f32[160,128]{1,0:T(8,128)S(1)}, f32[160,128]{1,0:T(8,128)S(1)}, u32[]{:S(2)}, u32[]{:S(2)}) %collective-permute-start.15) | collective-permute-done | bytes 81952 | tf_op jit(solution)/shard_map/ppermute | solution.py:23
  62.2 2.2 %collective-permute-done.16 = f32[160,128]{1,0:T(8,128)S(1)} collective-permute-done((f32[160,128]{1,0:T(8,128)S(1)}, f32[160,128]{1,0:T(8,128)S(1)}, u32[]{:S(2)}, u32[]{:S(2)}) %collective-permute-start.16) | collective-permute-done | bytes 81952 | tf_op jit(solution)/shard_map/ppermute | solution.py:23
  64.4 1.7 %shard_map.37 = (bf16[512,1024]{1,0:T(8,128)(2,1)S(1)}, bf16[512,512]{1,0:T(8,128)(2,1)S(1)}, bf16[512,512]{1,0:T(8,128)(2,1)S(1)}, bf16[256,512]{1,0:T(8,128)(2,1)S(1)}) custom-call(s32[3]{0:T(128)S(1)} %pad_add_fusion.where, f32[128,1024]{1,0:T(8,128)S(1)} %get-tuple-element.35.own, f32[128,1024]{1,0:T(8,128)S(1)} %collective-permute-done.1.refs_0_, ...), custom_call_target="tpu_custom_call" | custom-call | flops 805306368 | bytes 4456460 | tf_op jit(solution)/shard_map/pallas_call | solution.py:28
  66.3 5.4 %shard_map.39 = (f32[4,64,1024]{2,1,0:T(8,128)S(1)}, f32[64,1024]{1,0:T(8,128)S(1)}, f32[64,1024]{1,0:T(8,128)S(1)}, f32[64,1024]{1,0:T(8,128)S(1)}) fusion(f32[4,64,1024]{2,1,0:T(8,128)S(1)} %broadcast_in_dim.22, s32[]{:T(128)S(6)} %select_n.54, s32[3]{0:T(128)S(1)} %pad_add_fusion.where, bf16[512,1024]{1,0:T(8,128)(2,1)S(1)} %get-tuple-element.15, ...), kind=kCustom, calls=%fused_computation.8 | custom fusion | bytes 4063748 | tf_op jit(solution)/shard_map/pallas_call | solution.py:28
  71.8 1.3 %collective-permute-start.21 = (f32[64,1024]{1,0:T(8,128)S(1)}, f32[64,1024]{1,0:T(8,128)S(1)}, u32[]{:S(2)}, u32[]{:S(2)}) collective-permute-start(f32[64,1024]{1,0:T(8,128)S(1)} %get-tuple-element.28), channel_id=1, source_target_pairs={{0,8},{8,0},{16,24},{24,16},{1,9},{9,1},{17,25},{25,17},{2,10},{10... | collective-permute-start | bytes 786440 | tf_op jit(solution)/shard_map/ppermute | solution.py:229
  73.9 1.4 %collective-permute-start.23 = (f32[64,1024]{1,0:T(8,128)S(1)}, f32[64,1024]{1,0:T(8,128)S(1)}, u32[]{:S(2)}, u32[]{:S(2)}) collective-permute-start(f32[64,1024]{1,0:T(8,128)S(1)} %get-tuple-element.32), channel_id=1, source_target_pairs={{0,24},{8,16},{16,8},{24,0},{1,25},{9,17},{17,9},{25,1},{2,26},{10... | collective-permute-start | bytes 786440 | tf_op jit(solution)/shard_map/ppermute | solution.py:229
  75.3 5.7 %collective-permute-done.21 = f32[64,1024]{1,0:T(8,128)S(1)} collective-permute-done((f32[64,1024]{1,0:T(8,128)S(1)}, f32[64,1024]{1,0:T(8,128)S(1)}, u32[]{:S(2)}, u32[]{:S(2)}) %collective-permute-start.21) | collective-permute-done | bytes 262176 | tf_op jit(solution)/shard_map/ppermute | solution.py:229
  81.0 4.5 %collective-permute-done.22 = f32[64,1024]{1,0:T(8,128)S(1)} collective-permute-done((f32[64,1024]{1,0:T(8,128)S(1)}, f32[64,1024]{1,0:T(8,128)S(1)}, u32[]{:S(2)}, u32[]{:S(2)}) %collective-permute-start.22) | collective-permute-done | bytes 262176 | tf_op jit(solution)/shard_map/ppermute | solution.py:229
  85.5 1.6 %collective-permute-done.23 = f32[64,1024]{1,0:T(8,128)S(1)} collective-permute-done((f32[64,1024]{1,0:T(8,128)S(1)}, f32[64,1024]{1,0:T(8,128)S(1)}, u32[]{:S(2)}, u32[]{:S(2)}) %collective-permute-start.23) | collective-permute-done | bytes 262176 | tf_op jit(solution)/shard_map/ppermute | solution.py:229
  (47 shorter events, 9.5 us)
Async XLA Ops:
  1.2 8.8 %collective-permute-start.4 = (f32[128,384]{1,0:T(8,128)S(1)}, f32[128,384]{1,0:T(8,128)S(1)}, u32[]{:S(2)}, u32[]{:S(2)}) collective-permute-start(f32[128,384]{1,0:T(8,128)S(1)} %get-tuple-element.38), channel_id=1, source_target_pairs={{0,8},{8,0},{16,24},{24,16},{1,9},{9,1},{17,25},{25,17},{2,10},{10... | collective-permute-start | bytes 589832 | tf_op jit(solution)/shard_map/ppermute | solution.py:23
  4.2 10.6 %collective-permute-start.5 = (f32[128,384]{1,0:T(8,128)S(1)}, f32[128,384]{1,0:T(8,128)S(1)}, u32[]{:S(2)}, u32[]{:S(2)}) collective-permute-start(f32[128,384]{1,0:T(8,128)S(1)} %get-tuple-element.40), channel_id=1, source_target_pairs={{0,16},{8,24},{16,0},{24,8},{1,17},{9,25},{17,1},{25,9},{2,18},{10... | collective-permute-start | bytes 589832 | tf_op jit(solution)/shard_map/ppermute | solution.py:23
  5.7 9.1 %collective-permute-start.6 = (f32[128,384]{1,0:T(8,128)S(1)}, f32[128,384]{1,0:T(8,128)S(1)}, u32[]{:S(2)}, u32[]{:S(2)}) collective-permute-start(f32[128,384]{1,0:T(8,128)S(1)} %get-tuple-element.37), channel_id=1, source_target_pairs={{0,24},{8,16},{16,8},{24,0},{1,25},{9,17},{17,9},{25,1},{2,26},{10... | collective-permute-start | bytes 589832 | tf_op jit(solution)/shard_map/ppermute | solution.py:23
  6.1 9.9 %collective-permute-start = (f32[1,128]{1,0:T(1,128)S(1)}, f32[1,128]{1,0:T(1,128)S(1)}, u32[]{:S(2)}, u32[]{:S(2)}) collective-permute-start(f32[1,128]{1,0:T(1,128)S(1)} %bitcast.15), channel_id=1, source_target_pairs={{0,4},{4,0},{1,5},{5,1},{2,6},{6,2},{3,7},{7,3},{8,12},{12,8},{9,1... | collective-permute-start | bytes 1544 | tf_op jit(solution)/shard_map/ppermute | solution.py:23
  15.9 1.7 %collective-permute-start.7 = (f32[640,128]{1,0:T(8,128)S(1)}, f32[640,128]{1,0:T(8,128)S(1)}, u32[]{:S(2)}, u32[]{:S(2)}) collective-permute-start(f32[640,128]{1,0:T(8,128)S(1)} %get-tuple-element.20), channel_id=1, source_target_pairs={{0,4},{4,0},{1,5},{5,1},{2,6},{6,2},{3,7},{7,3},{8,12},{12,8},{9,1... | collective-permute-start | bytes 983048 | tf_op jit(solution)/shard_map/ppermute | solution.py:23
  17.6 7.3 %collective-permute-start.10 = (f32[160,128]{1,0:T(8,128)S(1)}, f32[160,128]{1,0:T(8,128)S(1)}, u32[]{:S(2)}, u32[]{:S(2)}) collective-permute-start(f32[160,128]{1,0:T(8,128)S(1)} %get-tuple-element.42), channel_id=1, source_target_pairs={{0,3},{1,2},{2,1},{3,0},{4,7},{5,6},{6,5},{7,4},{8,11},{9,10},{10,... | collective-permute-start | bytes 245768 | tf_op jit(solution)/shard_map/ppermute | solution.py:23
  21.3 6.2 %collective-permute-start.8 = (f32[160,128]{1,0:T(8,128)S(1)}, f32[160,128]{1,0:T(8,128)S(1)}, u32[]{:S(2)}, u32[]{:S(2)}) collective-permute-start(f32[160,128]{1,0:T(8,128)S(1)} %get-tuple-element.43), channel_id=1, source_target_pairs={{0,1},{1,0},{2,3},{3,2},{4,5},{5,4},{6,7},{7,6},{8,9},{9,8},{10,11... | collective-permute-start | bytes 245768 | tf_op jit(solution)/shard_map/ppermute | solution.py:23
  21.3 7.2 %collective-permute-start.9 = (f32[160,128]{1,0:T(8,128)S(1)}, f32[160,128]{1,0:T(8,128)S(1)}, u32[]{:S(2)}, u32[]{:S(2)}) collective-permute-start(f32[160,128]{1,0:T(8,128)S(1)} %get-tuple-element.41), channel_id=1, source_target_pairs={{0,2},{1,3},{2,0},{3,1},{4,6},{5,7},{6,4},{7,5},{8,10},{9,11},{10,... | collective-permute-start | bytes 245768 | tf_op jit(solution)/shard_map/ppermute | solution.py:23
  22.4 35.8 %collective-permute-start.1 = (f32[128,1024]{1,0:T(8,128)S(1)}, f32[128,1024]{1,0:T(8,128)S(1)}, u32[]{:S(2)}, u32[]{:S(2)}) collective-permute-start(f32[128,1024]{1,0:T(8,128)S(1)} %get-tuple-element.34), channel_id=1, source_target_pairs={{0,8},{8,0},{16,24},{24,16},{1,9},{9,1},{17,25},{25,17},{2,10},{10... | collective-permute-start | bytes 1572872 | tf_op jit(solution)/shard_map/ppermute | solution.py:23
  23.7 34.9 %collective-permute-start.2 = (f32[128,1024]{1,0:T(8,128)S(1)}, f32[128,1024]{1,0:T(8,128)S(1)}, u32[]{:S(2)}, u32[]{:S(2)}) collective-permute-start(f32[128,1024]{1,0:T(8,128)S(1)} %get-tuple-element.36), channel_id=1, source_target_pairs={{0,16},{8,24},{16,0},{24,8},{1,17},{9,25},{17,1},{25,9},{2,18},{10... | collective-permute-start | bytes 1572872 | tf_op jit(solution)/shard_map/ppermute | solution.py:23
  24.9 39.5 %collective-permute-start.3 = (f32[128,1024]{1,0:T(8,128)S(1)}, f32[128,1024]{1,0:T(8,128)S(1)}, u32[]{:S(2)}, u32[]{:S(2)}) collective-permute-start(f32[128,1024]{1,0:T(8,128)S(1)} %get-tuple-element.33), channel_id=1, source_target_pairs={{0,24},{8,16},{16,8},{24,0},{1,25},{9,17},{17,9},{25,1},{2,26},{10... | collective-permute-start | bytes 1572872 | tf_op jit(solution)/shard_map/ppermute | solution.py:23
  28.5 20.2 %collective-permute-start.11 = (f32[160,128]{1,0:T(8,128)S(1)}, f32[160,128]{1,0:T(8,128)S(1)}, u32[]{:S(2)}, u32[]{:S(2)}) collective-permute-start(f32[160,128]{1,0:T(8,128)S(1)} %slice_add_fusion), channel_id=1, source_target_pairs={{0,8},{8,0},{16,24},{24,16},{1,9},{9,1},{17,25},{25,17},{2,10},{10... | collective-permute-start | bytes 245768 | tf_op jit(solution)/shard_map/ppermute | solution.py:23
  29.8 20.4 %collective-permute-start.12 = (f32[160,128]{1,0:T(8,128)S(1)}, f32[160,128]{1,0:T(8,128)S(1)}, u32[]{:S(2)}, u32[]{:S(2)}) collective-permute-start(f32[160,128]{1,0:T(8,128)S(1)} %slice_add_fusion), channel_id=1, source_target_pairs={{0,16},{8,24},{16,0},{24,8},{1,17},{9,25},{17,1},{25,9},{2,18},{10... | collective-permute-start | bytes 245768 | tf_op jit(solution)/shard_map/ppermute | solution.py:23
  48.7 5.3 %collective-permute-start.13 = (f32[160,128]{1,0:T(8,128)S(1)}, f32[160,128]{1,0:T(8,128)S(1)}, u32[]{:S(2)}, u32[]{:S(2)}) collective-permute-start(f32[160,128]{1,0:T(8,128)S(1)} %slice_add_fusion), channel_id=1, source_target_pairs={{0,24},{8,16},{16,8},{24,0},{1,25},{9,17},{17,9},{25,1},{2,26},{10... | collective-permute-start | bytes 245768 | tf_op jit(solution)/shard_map/ppermute | solution.py:23
  54.1 4.7 %collective-permute-start.14 = (f32[160,128]{1,0:T(8,128)S(1)}, f32[160,128]{1,0:T(8,128)S(1)}, u32[]{:S(2)}, u32[]{:S(2)}) collective-permute-start(f32[160,128]{1,0:T(8,128)S(1)} %add_add_fusion), channel_id=1, source_target_pairs={{0,1},{1,0},{2,3},{3,2},{4,5},{5,4},{6,7},{7,6},{8,9},{9,8},{10,11... | collective-permute-start | bytes 245768 | tf_op jit(solution)/shard_map/ppermute | solution.py:23
  55.6 6.7 %collective-permute-start.15 = (f32[160,128]{1,0:T(8,128)S(1)}, f32[160,128]{1,0:T(8,128)S(1)}, u32[]{:S(2)}, u32[]{:S(2)}) collective-permute-start(f32[160,128]{1,0:T(8,128)S(1)} %add_add_fusion), channel_id=1, source_target_pairs={{0,2},{1,3},{2,0},{3,1},{4,6},{5,7},{6,4},{7,5},{8,10},{9,11},{10,... | collective-permute-start | bytes 245768 | tf_op jit(solution)/shard_map/ppermute | solution.py:23
  58.2 6.2 %collective-permute-start.16 = (f32[160,128]{1,0:T(8,128)S(1)}, f32[160,128]{1,0:T(8,128)S(1)}, u32[]{:S(2)}, u32[]{:S(2)}) collective-permute-start(f32[160,128]{1,0:T(8,128)S(1)} %add_add_fusion), channel_id=1, source_target_pairs={{0,3},{1,2},{2,1},{3,0},{4,7},{5,6},{6,5},{7,4},{8,11},{9,10},{10,... | collective-permute-start | bytes 245768 | tf_op jit(solution)/shard_map/ppermute | solution.py:23
  58.6 7.6 %collective-permute-start.17 = (f32[160,128]{1,0:T(8,128)S(1)}, f32[160,128]{1,0:T(8,128)S(1)}, u32[]{:S(2)}, u32[]{:S(2)}) collective-permute-start(f32[160,128]{1,0:T(8,128)S(1)} %add_add_fusion), channel_id=1, source_target_pairs={{0,4},{4,0},{1,5},{5,1},{2,6},{6,2},{3,7},{7,3},{8,12},{12,8},{9,1... | collective-permute-start | bytes 245768 | tf_op jit(solution)/shard_map/ppermute | solution.py:23
  58.8 7.4 %collective-permute-start.18 = (f32[160,128]{1,0:T(8,128)S(1)}, f32[160,128]{1,0:T(8,128)S(1)}, u32[]{:S(2)}, u32[]{:S(2)}) collective-permute-start(f32[160,128]{1,0:T(8,128)S(1)} %collective-permute-done.14), channel_id=1, source_target_pairs={{0,4},{4,0},{1,5},{5,1},{2,6},{6,2},{3,7},{7,3},{8,12},{12,8},{9,1... | collective-permute-start | bytes 245768 | tf_op jit(solution)/shard_map/ppermute | solution.py:23
  62.2 4.0 %collective-permute-start.19 = (f32[160,128]{1,0:T(8,128)S(1)}, f32[160,128]{1,0:T(8,128)S(1)}, u32[]{:S(2)}, u32[]{:S(2)}) collective-permute-start(f32[160,128]{1,0:T(8,128)S(1)} %collective-permute-done.15), channel_id=1, source_target_pairs={{0,4},{4,0},{1,5},{5,1},{2,6},{6,2},{3,7},{7,3},{8,12},{12,8},{9,1... | collective-permute-start | bytes 245768 | tf_op jit(solution)/shard_map/ppermute | solution.py:23
  64.4 1.8 %collective-permute-start.20 = (f32[160,128]{1,0:T(8,128)S(1)}, f32[160,128]{1,0:T(8,128)S(1)}, u32[]{:S(2)}, u32[]{:S(2)}) collective-permute-start(f32[160,128]{1,0:T(8,128)S(1)} %collective-permute-done.16), channel_id=1, source_target_pairs={{0,4},{4,0},{1,5},{5,1},{2,6},{6,2},{3,7},{7,3},{8,12},{12,8},{9,1... | collective-permute-start | bytes 245768 | tf_op jit(solution)/shard_map/ppermute | solution.py:23
  71.8 9.2 %collective-permute-start.21 = (f32[64,1024]{1,0:T(8,128)S(1)}, f32[64,1024]{1,0:T(8,128)S(1)}, u32[]{:S(2)}, u32[]{:S(2)}) collective-permute-start(f32[64,1024]{1,0:T(8,128)S(1)} %get-tuple-element.28), channel_id=1, source_target_pairs={{0,8},{8,0},{16,24},{24,16},{1,9},{9,1},{17,25},{25,17},{2,10},{10... | collective-permute-start | bytes 786440 | tf_op jit(solution)/shard_map/ppermute | solution.py:229
  73.1 12.4 %collective-permute-start.22 = (f32[64,1024]{1,0:T(8,128)S(1)}, f32[64,1024]{1,0:T(8,128)S(1)}, u32[]{:S(2)}, u32[]{:S(2)}) collective-permute-start(f32[64,1024]{1,0:T(8,128)S(1)} %get-tuple-element.30), channel_id=1, source_target_pairs={{0,16},{8,24},{16,0},{24,8},{1,17},{9,25},{17,1},{25,9},{2,18},{10... | collective-permute-start | bytes 786440 | tf_op jit(solution)/shard_map/ppermute | solution.py:229
  73.9 13.2 %collective-permute-start.23 = (f32[64,1024]{1,0:T(8,128)S(1)}, f32[64,1024]{1,0:T(8,128)S(1)}, u32[]{:S(2)}, u32[]{:S(2)}) collective-permute-start(f32[64,1024]{1,0:T(8,128)S(1)} %get-tuple-element.32), channel_id=1, source_target_pairs={{0,24},{8,16},{16,8},{24,0},{1,25},{9,17},{17,9},{25,1},{2,26},{10... | collective-permute-start | bytes 786440 | tf_op jit(solution)/shard_map/ppermute | solution.py:229
  (3 other events, 22.2 us)

commit v3 on v2

--- a/solution.py
+++ b/solution.py
@@ -8,6 +8,7 @@
 from jax.sharding import PartitionSpec as P
 
 BLK = 1024
+
 
 epsilon = 1e-06
 damping = 0.01
@@ -172,8 +173,9 @@
         scale = lax.dynamic_slice_in_dim(gain, at, BLK, 0).astype(f32)
         return part * inverse * scale
 
-    normed_parts = [swap(normed_part(me ^ by), "dp", by) for by in range(1, dp)]
-    normed_parts = [normed_part(me)] + normed_parts
+    normed_parts = [normed_part(me)]
+    for by in range(1, dp):
+        normed_parts.append(swap(normed_part(me ^ by), "dp", by))
 
     tiles = dp * (dp + 1) // 2
     piece = -(-tiles * size // (nten * npre * 8)) * 8

time: 88 us -> 88 us (level)
  no operation moved by 1% of the time
where the time goes in v3:
time: 88 us; the launch traced here: 87.9 us
  waiting for transfers between devices  51.9 us (59%)
  starting transfers between devices  24.7 us (28%)
  local copies, waits for them, and re-layouts  6.35 us (7%)
  Pallas kernels  2.77 us (3%)
  other arithmetic  1.91 us (2%)
    ppermute x21, waiting for transfers between devices, swap(): return lax.ppermute(value, axis, [(i, i ^ by) for i in range(size)])  40.2 us
    ppermute x21, starting transfers between devices, swap(): return lax.ppermute(value, axis, [(i, i ^ by) for i in range(size)])  21.1 us
    ppermute x3, waiting for transfers between devices, program(): sent = lax.ppermute(sent, 'dp', pairs)  11.7 us
    pallas_call x1, local copies, waits for them, and re-layouts, call(): pl.pallas_call(kernel, out_shape=list(outs), in_specs=[SMEM] + [VMEM] * (...  5.45 us
    ppermute x3, starting transfers between devices, program(): sent = lax.ppermute(sent, 'dp', pairs)  3.55 us
    pallas_call x2, Pallas kernels, call(): pl.pallas_call(kernel, out_shape=list(outs), in_specs=[SMEM] + [VMEM] * (...  2.77 us
  transfers between devices with their start and end apart: 24, of which 14 were waited for; matrix products, arithmetic and copies ran while one was open for 1% of the time, Pallas kernels for 3%

profile of v3, /device:TPU:0, one launch (start us, length us, event | category | flops | bytes accessed | tf_op | source)
XLA Modules:
  0.0 87.9 jit_solution(6101503287692464862)
XLA Ops:
  0.0 1.2 %dynamic-slice_convert_fusion = (f32[128,384]{1,0:T(8,128)S(1)}, f32[128,384]{1,0:T(8,128)S(1)}, bf16[128,384]{1,0:T(8,128)(2,1)S(1)}, f32[128,384]{1,0:T(8,128)S(1)}) fusion(bf16[128,3072]{1,0:T(8,128)(2,1)} %param.5, s32[]{:T(128)S(6)} %select_n.53, s32[]{:T(128)S(6)} %select_n.51, s32[]{:T(128)S(6)} %select_n.50, s32[]{:T(128)S(6)} %select_n.52), kind=kLoop, calls=%fused_computation.9 | loop fusion | flops 147456 | bytes 1081360 | tf_op jit(solution)/shard_map/convert_element_type | solution.py:162
  1.2 3.0 %collective-permute-start.4 = (f32[128,384]{1,0:T(8,128)S(1)}, f32[128,384]{1,0:T(8,128)S(1)}, u32[]{:S(2)}, u32[]{:S(2)}) collective-permute-start(f32[128,384]{1,0:T(8,128)S(1)} %get-tuple-element.38), channel_id=1, source_target_pairs={{0,8},{8,0},{16,24},{24,16},{1,9},{9,1},{17,25},{25,17},{2,10},{10... | collective-permute-start | bytes 589832 | tf_op jit(solution)/shard_map/ppermute | solution.py:24
  4.2 1.5 %collective-permute-start.5 = (f32[128,384]{1,0:T(8,128)S(1)}, f32[128,384]{1,0:T(8,128)S(1)}, u32[]{:S(2)}, u32[]{:S(2)}) collective-permute-start(f32[128,384]{1,0:T(8,128)S(1)} %get-tuple-element.40), channel_id=1, source_target_pairs={{0,16},{8,24},{16,0},{24,8},{1,17},{9,25},{17,1},{25,9},{2,18},{10... | collective-permute-start | bytes 589832 | tf_op jit(solution)/shard_map/ppermute | solution.py:24
  6.2 3.7 %collective-permute-done.4.refs_0_ = f32[128,384]{1,0:T(8,128)S(1)} collective-permute-done((f32[128,384]{1,0:T(8,128)S(1)}, f32[128,384]{1,0:T(8,128)S(1)}, u32[]{:S(2)}, u32[]{:S(2)}) %collective-permute-start.4) | collective-permute-done | bytes 196640 | tf_op jit(solution)/shard_map/ppermute | solution.py:24
  10.0 4.8 %collective-permute-done.5.refs_1_ = f32[128,384]{1,0:T(8,128)S(1)} collective-permute-done((f32[128,384]{1,0:T(8,128)S(1)}, f32[128,384]{1,0:T(8,128)S(1)}, u32[]{:S(2)}, u32[]{:S(2)}) %collective-permute-start.5) | collective-permute-done | bytes 196640 | tf_op jit(solution)/shard_map/ppermute | solution.py:24
  16.0 1.6 %collective-permute-done.7 = f32[640,128]{1,0:T(8,128)S(1)} collective-permute-done((f32[640,128]{1,0:T(8,128)S(1)}, f32[640,128]{1,0:T(8,128)S(1)}, u32[]{:S(2)}, u32[]{:S(2)}) %collective-permute-start.7) | collective-permute-done | bytes 327712 | tf_op jit(solution)/shard_map/ppermute | solution.py:24
  17.6 3.7 %collective-permute-start.10 = (f32[160,128]{1,0:T(8,128)S(1)}, f32[160,128]{1,0:T(8,128)S(1)}, u32[]{:S(2)}, u32[]{:S(2)}) collective-permute-start(f32[160,128]{1,0:T(8,128)S(1)} %get-tuple-element.42), channel_id=1, source_target_pairs={{0,3},{1,2},{2,1},{3,0},{4,7},{5,6},{6,5},{7,4},{8,11},{9,10},{10,... | collective-permute-start | bytes 245768 | tf_op jit(solution)/shard_map/ppermute | solution.py:24
  22.4 1.3 %collective-permute-start.1 = (f32[128,1024]{1,0:T(8,128)S(1)}, f32[128,1024]{1,0:T(8,128)S(1)}, u32[]{:S(2)}, u32[]{:S(2)}) collective-permute-start(f32[128,1024]{1,0:T(8,128)S(1)} %get-tuple-element.34), channel_id=1, source_target_pairs={{0,8},{8,0},{16,24},{24,16},{1,9},{9,1},{17,25},{25,17},{2,10},{10... | collective-permute-start | bytes 1572872 | tf_op jit(solution)/shard_map/ppermute | solution.py:24
  24.9 1.5 %collective-permute-start.3 = (f32[128,1024]{1,0:T(8,128)S(1)}, f32[128,1024]{1,0:T(8,128)S(1)}, u32[]{:S(2)}, u32[]{:S(2)}) collective-permute-start(f32[128,1024]{1,0:T(8,128)S(1)} %get-tuple-element.33), channel_id=1, source_target_pairs={{0,24},{8,16},{16,8},{24,0},{1,25},{9,17},{17,9},{25,1},{2,26},{10... | collective-permute-start | bytes 1572872 | tf_op jit(solution)/shard_map/ppermute | solution.py:24
  28.5 1.3 %collective-permute-start.11 = (f32[160,128]{1,0:T(8,128)S(1)}, f32[160,128]{1,0:T(8,128)S(1)}, u32[]{:S(2)}, u32[]{:S(2)}) collective-permute-start(f32[160,128]{1,0:T(8,128)S(1)} %slice_add_fusion), channel_id=1, source_target_pairs={{0,8},{8,0},{16,24},{24,16},{1,9},{9,1},{17,25},{25,17},{2,10},{10... | collective-permute-start | bytes 245768 | tf_op jit(solution)/shard_map/ppermute | solution.py:24
  30.6 18.1 %collective-permute-done.11 = f32[160,128]{1,0:T(8,128)S(1)} collective-permute-done((f32[160,128]{1,0:T(8,128)S(1)}, f32[160,128]{1,0:T(8,128)S(1)}, u32[]{:S(2)}, u32[]{:S(2)}) %collective-permute-start.11) | collective-permute-done | bytes 81952 | tf_op jit(solution)/shard_map/ppermute | solution.py:24
  48.7 1.5 %collective-permute-start.13 = (f32[160,128]{1,0:T(8,128)S(1)}, f32[160,128]{1,0:T(8,128)S(1)}, u32[]{:S(2)}, u32[]{:S(2)}) collective-permute-start(f32[160,128]{1,0:T(8,128)S(1)} %slice_add_fusion), channel_id=1, source_target_pairs={{0,24},{8,16},{16,8},{24,0},{1,25},{9,17},{17,9},{25,1},{2,26},{10... | collective-permute-start | bytes 245768 | tf_op jit(solution)/shard_map/ppermute | solution.py:24
  50.2 3.8 %collective-permute-done.13 = f32[160,128]{1,0:T(8,128)S(1)} collective-permute-done((f32[160,128]{1,0:T(8,128)S(1)}, f32[160,128]{1,0:T(8,128)S(1)}, u32[]{:S(2)}, u32[]{:S(2)}) %collective-permute-start.13) | collective-permute-done | bytes 81952 | tf_op jit(solution)/shard_map/ppermute | solution.py:24
  54.1 1.5 %collective-permute-start.14 = (f32[160,128]{1,0:T(8,128)S(1)}, f32[160,128]{1,0:T(8,128)S(1)}, u32[]{:S(2)}, u32[]{:S(2)}) collective-permute-start(f32[160,128]{1,0:T(8,128)S(1)} %add_add_fusion), channel_id=1, source_target_pairs={{0,1},{1,0},{2,3},{3,2},{4,5},{5,4},{6,7},{7,6},{8,9},{9,8},{10,11... | collective-permute-start | bytes 245768 | tf_op jit(solution)/shard_map/ppermute | solution.py:24
  55.6 2.6 %collective-permute-start.15 = (f32[160,128]{1,0:T(8,128)S(1)}, f32[160,128]{1,0:T(8,128)S(1)}, u32[]{:S(2)}, u32[]{:S(2)}) collective-permute-start(f32[160,128]{1,0:T(8,128)S(1)} %add_add_fusion), channel_id=1, source_target_pairs={{0,2},{1,3},{2,0},{3,1},{4,6},{5,7},{6,4},{7,5},{8,10},{9,11},{10,... | collective-permute-start | bytes 245768 | tf_op jit(solution)/shard_map/ppermute | solution.py:24
  59.1 3.2 %collective-permute-done.15 = f32[160,128]{1,0:T(8,128)S(1)} collective-permute-done((f32[160,128]{1,0:T(8,128)S(1)}, f32[160,128]{1,0:T(8,128)S(1)}, u32[]{:S(2)}, u32[]{:S(2)}) %collective-permute-start.15) | collective-permute-done | bytes 81952 | tf_op jit(solution)/shard_map/ppermute | solution.py:24
  62.2 2.2 %collective-permute-done.16 = f32[160,128]{1,0:T(8,128)S(1)} collective-permute-done((f32[160,128]{1,0:T(8,128)S(1)}, f32[160,128]{1,0:T(8,128)S(1)}, u32[]{:S(2)}, u32[]{:S(2)}) %collective-permute-start.16) | collective-permute-done | bytes 81952 | tf_op jit(solution)/shard_map/ppermute | solution.py:24
  64.4 1.7 %shard_map.37 = (bf16[512,1024]{1,0:T(8,128)(2,1)S(1)}, bf16[512,512]{1,0:T(8,128)(2,1)S(1)}, bf16[512,512]{1,0:T(8,128)(2,1)S(1)}, bf16[256,512]{1,0:T(8,128)(2,1)S(1)}) custom-call(s32[3]{0:T(128)S(1)} %pad_add_fusion.where, f32[128,1024]{1,0:T(8,128)S(1)} %get-tuple-element.35.own, f32[128,1024]{1,0:T(8,128)S(1)} %collective-permute-done.1.refs_0_, ...), custom_call_target="tpu_custom_call" | custom-call | flops 805306368 | bytes 4456460 | tf_op jit(solution)/shard_map/pallas_call | solution.py:29
  66.3 5.4 %shard_map.39 = (f32[4,64,1024]{2,1,0:T(8,128)S(1)}, f32[64,1024]{1,0:T(8,128)S(1)}, f32[64,1024]{1,0:T(8,128)S(1)}, f32[64,1024]{1,0:T(8,128)S(1)}) fusion(f32[4,64,1024]{2,1,0:T(8,128)S(1)} %broadcast_in_dim.22, s32[]{:T(128)S(6)} %select_n.54, s32[3]{0:T(128)S(1)} %pad_add_fusion.where, bf16[512,1024]{1,0:T(8,128)(2,1)S(1)} %get-tuple-element.15, ...), kind=kCustom, calls=%fused_computation.8 | custom fusion | bytes 4063748 | tf_op jit(solution)/shard_map/pallas_call | solution.py:29
  71.8 1.3 %collective-permute-start.21 = (f32[64,1024]{1,0:T(8,128)S(1)}, f32[64,1024]{1,0:T(8,128)S(1)}, u32[]{:S(2)}, u32[]{:S(2)}) collective-permute-start(f32[64,1024]{1,0:T(8,128)S(1)} %get-tuple-element.28), channel_id=1, source_target_pairs={{0,8},{8,0},{16,24},{24,16},{1,9},{9,1},{17,25},{25,17},{2,10},{10... | collective-permute-start | bytes 786440 | tf_op jit(solution)/shard_map/ppermute | solution.py:231
  73.9 1.4 %collective-permute-start.23 = (f32[64,1024]{1,0:T(8,128)S(1)}, f32[64,1024]{1,0:T(8,128)S(1)}, u32[]{:S(2)}, u32[]{:S(2)}) collective-permute-start(f32[64,1024]{1,0:T(8,128)S(1)} %get-tuple-element.32), channel_id=1, source_target_pairs={{0,24},{8,16},{16,8},{24,0},{1,25},{9,17},{17,9},{25,1},{2,26},{10... | collective-permute-start | bytes 786440 | tf_op jit(solution)/shard_map/ppermute | solution.py:231
  75.3 5.7 %collective-permute-done.21 = f32[64,1024]{1,0:T(8,128)S(1)} collective-permute-done((f32[64,1024]{1,0:T(8,128)S(1)}, f32[64,1024]{1,0:T(8,128)S(1)}, u32[]{:S(2)}, u32[]{:S(2)}) %collective-permute-start.21) | collective-permute-done | bytes 262176 | tf_op jit(solution)/shard_map/ppermute | solution.py:231
  81.0 4.5 %collective-permute-done.22 = f32[64,1024]{1,0:T(8,128)S(1)} collective-permute-done((f32[64,1024]{1,0:T(8,128)S(1)}, f32[64,1024]{1,0:T(8,128)S(1)}, u32[]{:S(2)}, u32[]{:S(2)}) %collective-permute-start.22) | collective-permute-done | bytes 262176 | tf_op jit(solution)/shard_map/ppermute | solution.py:231
  85.5 1.6 %collective-permute-done.23 = f32[64,1024]{1,0:T(8,128)S(1)} collective-permute-done((f32[64,1024]{1,0:T(8,128)S(1)}, f32[64,1024]{1,0:T(8,128)S(1)}, u32[]{:S(2)}, u32[]{:S(2)}) %collective-permute-start.23) | collective-permute-done | bytes 262176 | tf_op jit(solution)/shard_map/ppermute | solution.py:231
  (47 shorter events, 9.5 us)
Async XLA Ops:
  1.2 8.8 %collective-permute-start.4 = (f32[128,384]{1,0:T(8,128)S(1)}, f32[128,384]{1,0:T(8,128)S(1)}, u32[]{:S(2)}, u32[]{:S(2)}) collective-permute-start(f32[128,384]{1,0:T(8,128)S(1)} %get-tuple-element.38), channel_id=1, source_target_pairs={{0,8},{8,0},{16,24},{24,16},{1,9},{9,1},{17,25},{25,17},{2,10},{10... | collective-permute-start | bytes 589832 | tf_op jit(solution)/shard_map/ppermute | solution.py:24
  4.2 10.6 %collective-permute-start.5 = (f32[128,384]{1,0:T(8,128)S(1)}, f32[128,384]{1,0:T(8,128)S(1)}, u32[]{:S(2)}, u32[]{:S(2)}) collective-permute-start(f32[128,384]{1,0:T(8,128)S(1)} %get-tuple-element.40), channel_id=1, source_target_pairs={{0,16},{8,24},{16,0},{24,8},{1,17},{9,25},{17,1},{25,9},{2,18},{10... | collective-permute-start | bytes 589832 | tf_op jit(solution)/shard_map/ppermute | solution.py:24
  5.7 9.1 %collective-permute-start.6 = (f32[128,384]{1,0:T(8,128)S(1)}, f32[128,384]{1,0:T(8,128)S(1)}, u32[]{:S(2)}, u32[]{:S(2)}) collective-permute-start(f32[128,384]{1,0:T(8,128)S(1)} %get-tuple-element.37), channel_id=1, source_target_pairs={{0,24},{8,16},{16,8},{24,0},{1,25},{9,17},{17,9},{25,1},{2,26},{10... | collective-permute-start | bytes 589832 | tf_op jit(solution)/shard_map/ppermute | solution.py:24
  6.1 9.9 %collective-permute-start = (f32[1,128]{1,0:T(1,128)S(1)}, f32[1,128]{1,0:T(1,128)S(1)}, u32[]{:S(2)}, u32[]{:S(2)}) collective-permute-start(f32[1,128]{1,0:T(1,128)S(1)} %bitcast.15), channel_id=1, source_target_pairs={{0,4},{4,0},{1,5},{5,1},{2,6},{6,2},{3,7},{7,3},{8,12},{12,8},{9,1... | collective-permute-start | bytes 1544 | tf_op jit(solution)/shard_map/ppermute | solution.py:24
  15.9 1.7 %collective-permute-start.7 = (f32[640,128]{1,0:T(8,128)S(1)}, f32[640,128]{1,0:T(8,128)S(1)}, u32[]{:S(2)}, u32[]{:S(2)}) collective-permute-start(f32[640,128]{1,0:T(8,128)S(1)} %get-tuple-element.20), channel_id=1, source_target_pairs={{0,4},{4,0},{1,5},{5,1},{2,6},{6,2},{3,7},{7,3},{8,12},{12,8},{9,1... | collective-permute-start | bytes 983048 | tf_op jit(solution)/shard_map/ppermute | solution.py:24
  17.6 7.3 %collective-permute-start.10 = (f32[160,128]{1,0:T(8,128)S(1)}, f32[160,128]{1,0:T(8,128)S(1)}, u32[]{:S(2)}, u32[]{:S(2)}) collective-permute-start(f32[160,128]{1,0:T(8,128)S(1)} %get-tuple-element.42), channel_id=1, source_target_pairs={{0,3},{1,2},{2,1},{3,0},{4,7},{5,6},{6,5},{7,4},{8,11},{9,10},{10,... | collective-permute-start | bytes 245768 | tf_op jit(solution)/shard_map/ppermute | solution.py:24
  21.3 6.2 %collective-permute-start.8 = (f32[160,128]{1,0:T(8,128)S(1)}, f32[160,128]{1,0:T(8,128)S(1)}, u32[]{:S(2)}, u32[]{:S(2)}) collective-permute-start(f32[160,128]{1,0:T(8,128)S(1)} %get-tuple-element.43), channel_id=1, source_target_pairs={{0,1},{1,0},{2,3},{3,2},{4,5},{5,4},{6,7},{7,6},{8,9},{9,8},{10,11... | collective-permute-start | bytes 245768 | tf_op jit(solution)/shard_map/ppermute | solution.py:24
  21.3 7.2 %collective-permute-start.9 = (f32[160,128]{1,0:T(8,128)S(1)}, f32[160,128]{1,0:T(8,128)S(1)}, u32[]{:S(2)}, u32[]{:S(2)}) collective-permute-start(f32[160,128]{1,0:T(8,128)S(1)} %get-tuple-element.41), channel_id=1, source_target_pairs={{0,2},{1,3},{2,0},{3,1},{4,6},{5,7},{6,4},{7,5},{8,10},{9,11},{10,... | collective-permute-start | bytes 245768 | tf_op jit(solution)/shard_map/ppermute | solution.py:24
  22.4 35.8 %collective-permute-start.1 = (f32[128,1024]{1,0:T(8,128)S(1)}, f32[128,1024]{1,0:T(8,128)S(1)}, u32[]{:S(2)}, u32[]{:S(2)}) collective-permute-start(f32[128,1024]{1,0:T(8,128)S(1)} %get-tuple-element.34), channel_id=1, source_target_pairs={{0,8},{8,0},{16,24},{24,16},{1,9},{9,1},{17,25},{25,17},{2,10},{10... | collective-permute-start | bytes 1572872 | tf_op jit(solution)/shard_map/ppermute | solution.py:24
  23.7 34.9 %collective-permute-start.2 = (f32[128,1024]{1,0:T(8,128)S(1)}, f32[128,1024]{1,0:T(8,128)S(1)}, u32[]{:S(2)}, u32[]{:S(2)}) collective-permute-start(f32[128,1024]{1,0:T(8,128)S(1)} %get-tuple-element.36), channel_id=1, source_target_pairs={{0,16},{8,24},{16,0},{24,8},{1,17},{9,25},{17,1},{25,9},{2,18},{10... | collective-permute-start | bytes 1572872 | tf_op jit(solution)/shard_map/ppermute | solution.py:24
  24.9 39.5 %collective-permute-start.3 = (f32[128,1024]{1,0:T(8,128)S(1)}, f32[128,1024]{1,0:T(8,128)S(1)}, u32[]{:S(2)}, u32[]{:S(2)}) collective-permute-start(f32[128,1024]{1,0:T(8,128)S(1)} %get-tuple-element.33), channel_id=1, source_target_pairs={{0,24},{8,16},{16,8},{24,0},{1,25},{9,17},{17,9},{25,1},{2,26},{10... | collective-permute-start | bytes 1572872 | tf_op jit(solution)/shard_map/ppermute | solution.py:24
  28.5 20.2 %collective-permute-start.11 = (f32[160,128]{1,0:T(8,128)S(1)}, f32[160,128]{1,0:T(8,128)S(1)}, u32[]{:S(2)}, u32[]{:S(2)}) collective-permute-start(f32[160,128]{1,0:T(8,128)S(1)} %slice_add_fusion), channel_id=1, source_target_pairs={{0,8},{8,0},{16,24},{24,16},{1,9},{9,1},{17,25},{25,17},{2,10},{10... | collective-permute-start | bytes 245768 | tf_op jit(solution)/shard_map/ppermute | solution.py:24
  29.8 20.4 %collective-permute-start.12 = (f32[160,128]{1,0:T(8,128)S(1)}, f32[160,128]{1,0:T(8,128)S(1)}, u32[]{:S(2)}, u32[]{:S(2)}) collective-permute-start(f32[160,128]{1,0:T(8,128)S(1)} %slice_add_fusion), channel_id=1, source_target_pairs={{0,16},{8,24},{16,0},{24,8},{1,17},{9,25},{17,1},{25,9},{2,18},{10... | collective-permute-start | bytes 245768 | tf_op jit(solution)/shard_map/ppermute | solution.py:24
  48.7 5.3 %collective-permute-start.13 = (f32[160,128]{1,0:T(8,128)S(1)}, f32[160,128]{1,0:T(8,128)S(1)}, u32[]{:S(2)}, u32[]{:S(2)}) collective-permute-start(f32[160,128]{1,0:T(8,128)S(1)} %slice_add_fusion), channel_id=1, source_target_pairs={{0,24},{8,16},{16,8},{24,0},{1,25},{9,17},{17,9},{25,1},{2,26},{10... | collective-permute-start | bytes 245768 | tf_op jit(solution)/shard_map/ppermute | solution.py:24
  54.1 4.7 %collective-permute-start.14 = (f32[160,128]{1,0:T(8,128)S(1)}, f32[160,128]{1,0:T(8,128)S(1)}, u32[]{:S(2)}, u32[]{:S(2)}) collective-permute-start(f32[160,128]{1,0:T(8,128)S(1)} %add_add_fusion), channel_id=1, source_target_pairs={{0,1},{1,0},{2,3},{3,2},{4,5},{5,4},{6,7},{7,6},{8,9},{9,8},{10,11... | collective-permute-start | bytes 245768 | tf_op jit(solution)/shard_map/ppermute | solution.py:24
  55.6 6.7 %collective-permute-start.15 = (f32[160,128]{1,0:T(8,128)S(1)}, f32[160,128]{1,0:T(8,128)S(1)}, u32[]{:S(2)}, u32[]{:S(2)}) collective-permute-start(f32[160,128]{1,0:T(8,128)S(1)} %add_add_fusion), channel_id=1, source_target_pairs={{0,2},{1,3},{2,0},{3,1},{4,6},{5,7},{6,4},{7,5},{8,10},{9,11},{10,... | collective-permute-start | bytes 245768 | tf_op jit(solution)/shard_map/ppermute | solution.py:24
  58.2 6.2 %collective-permute-start.16 = (f32[160,128]{1,0:T(8,128)S(1)}, f32[160,128]{1,0:T(8,128)S(1)}, u32[]{:S(2)}, u32[]{:S(2)}) collective-permute-start(f32[160,128]{1,0:T(8,128)S(1)} %add_add_fusion), channel_id=1, source_target_pairs={{0,3},{1,2},{2,1},{3,0},{4,7},{5,6},{6,5},{7,4},{8,11},{9,10},{10,... | collective-permute-start | bytes 245768 | tf_op jit(solution)/shard_map/ppermute | solution.py:24
  58.6 7.6 %collective-permute-start.17 = (f32[160,128]{1,0:T(8,128)S(1)}, f32[160,128]{1,0:T(8,128)S(1)}, u32[]{:S(2)}, u32[]{:S(2)}) collective-permute-start(f32[160,128]{1,0:T(8,128)S(1)} %add_add_fusion), channel_id=1, source_target_pairs={{0,4},{4,0},{1,5},{5,1},{2,6},{6,2},{3,7},{7,3},{8,12},{12,8},{9,1... | collective-permute-start | bytes 245768 | tf_op jit(solution)/shard_map/ppermute | solution.py:24
  58.8 7.4 %collective-permute-start.18 = (f32[160,128]{1,0:T(8,128)S(1)}, f32[160,128]{1,0:T(8,128)S(1)}, u32[]{:S(2)}, u32[]{:S(2)}) collective-permute-start(f32[160,128]{1,0:T(8,128)S(1)} %collective-permute-done.14), channel_id=1, source_target_pairs={{0,4},{4,0},{1,5},{5,1},{2,6},{6,2},{3,7},{7,3},{8,12},{12,8},{9,1... | collective-permute-start | bytes 245768 | tf_op jit(solution)/shard_map/ppermute | solution.py:24
  62.2 4.0 %collective-permute-start.19 = (f32[160,128]{1,0:T(8,128)S(1)}, f32[160,128]{1,0:T(8,128)S(1)}, u32[]{:S(2)}, u32[]{:S(2)}) collective-permute-start(f32[160,128]{1,0:T(8,128)S(1)} %collective-permute-done.15), channel_id=1, source_target_pairs={{0,4},{4,0},{1,5},{5,1},{2,6},{6,2},{3,7},{7,3},{8,12},{12,8},{9,1... | collective-permute-start | bytes 245768 | tf_op jit(solution)/shard_map/ppermute | solution.py:24
  64.4 1.8 %collective-permute-start.20 = (f32[160,128]{1,0:T(8,128)S(1)}, f32[160,128]{1,0:T(8,128)S(1)}, u32[]{:S(2)}, u32[]{:S(2)}) collective-permute-start(f32[160,128]{1,0:T(8,128)S(1)} %collective-permute-done.16), channel_id=1, source_target_pairs={{0,4},{4,0},{1,5},{5,1},{2,6},{6,2},{3,7},{7,3},{8,12},{12,8},{9,1... | collective-permute-start | bytes 245768 | tf_op jit(solution)/shard_map/ppermute | solution.py:24
  71.8 9.2 %collective-permute-start.21 = (f32[64,1024]{1,0:T(8,128)S(1)}, f32[64,1024]{1,0:T(8,128)S(1)}, u32[]{:S(2)}, u32[]{:S(2)}) collective-permute-start(f32[64,1024]{1,0:T(8,128)S(1)} %get-tuple-element.28), channel_id=1, source_target_pairs={{0,8},{8,0},{16,24},{24,16},{1,9},{9,1},{17,25},{25,17},{2,10},{10... | collective-permute-start | bytes 786440 | tf_op jit(solution)/shard_map/ppermute | solution.py:231
  73.1 12.4 %collective-permute-start.22 = (f32[64,1024]{1,0:T(8,128)S(1)}, f32[64,1024]{1,0:T(8,128)S(1)}, u32[]{:S(2)}, u32[]{:S(2)}) collective-permute-start(f32[64,1024]{1,0:T(8,128)S(1)} %get-tuple-element.30), channel_id=1, source_target_pairs={{0,16},{8,24},{16,0},{24,8},{1,17},{9,25},{17,1},{25,9},{2,18},{10... | collective-permute-start | bytes 786440 | tf_op jit(solution)/shard_map/ppermute | solution.py:231
  73.9 13.2 %collective-permute-start.23 = (f32[64,1024]{1,0:T(8,128)S(1)}, f32[64,1024]{1,0:T(8,128)S(1)}, u32[]{:S(2)}, u32[]{:S(2)}) collective-permute-start(f32[64,1024]{1,0:T(8,128)S(1)} %get-tuple-element.32), channel_id=1, source_target_pairs={{0,24},{8,16},{16,8},{24,0},{1,25},{9,17},{17,9},{25,1},{2,26},{10... | collective-permute-start | bytes 786440 | tf_op jit(solution)/shard_map/ppermute | solution.py:231
  (3 other events, 22.2 us)

commit v4 on v3

--- a/solution.py
+++ b/solution.py
@@ -16,6 +16,7 @@
 f32 = jnp.float32
 bf16 = jnp.bfloat16
 VMEM = pl.BlockSpec(memory_space=pltpu.VMEM)
+ANY = pl.BlockSpec(memory_space=pl.ANY)
 SMEM = pl.BlockSpec(memory_space=pltpu.SMEM)
 
 
@@ -24,15 +25,15 @@
     return lax.ppermute(value, axis, [(i, i ^ by) for i in range(size)])
 
 
-def call(kernel, outs, *operands, scratch=(), flops=0):
+def call(kernel, outs, *operands, scratch=(), flops=0, vmem=16, out_spec=VMEM):
     moved = sum(a.size * a.dtype.itemsize for a in (*operands, *outs))
     return pl.pallas_call(
         kernel,
         out_shape=list(outs),
         in_specs=[SMEM] + [VMEM] * (len(operands) - 1),
-        out_specs=[VMEM] * len(outs),
+        out_specs=[out_spec] * len(outs),
         scratch_shapes=list(scratch),
-        compiler_params=pltpu.CompilerParams(vmem_limit_bytes=24 * 2**20),
+        compiler_params=pltpu.CompilerParams(vmem_limit_bytes=vmem * 2**20),
         cost_estimate=pl.CostEstimate(flops=flops, bytes_accessed=moved, transcendentals=0),
     )(*operands)
 
@@ -50,12 +51,26 @@
     return high, (value - high.astype(f32)).astype(bf16)
 
 
+def twice(left, right):
+    count = left[0].shape[0]
+    both = nn(jnp.concatenate(left, axis=0), right)
+    return both[:count] + both[count:]
+
+
 def product(left, right):
-    return nn(left[0], right[0]) + (nn(left[0], right[1]) + nn(left[1], right[0]))
+    return twice(left, right[0]) + nn(left[0], right[1])
 
 
 def rows_at(index, count):
     return pl.ds(pl.multiple_of(index * count, 8), count)
+
+
+def positions(size):
+    return tuple(lax.broadcasted_iota(jnp.int32, (size, size), axis) for axis in (0, 1))
+
+
+def packed_rows(dp, size):
+    return dp // 2 * size + dp * (dp - 1) // 2 * size + 8
 
 
 def gram_kernel(nten, npre, where, own, *refs):
@@ -65,14 +80,23 @@
     whole[rows_at(me, size)] = own[...].astype(bf16)
     for by, piece in enumerate(received, 1):
         whole[rows_at(me ^ by, size)] = piece[...].astype(bf16)
-    at = 0
+    down, across = positions(size)
+    even, at = None, dp // 2 * size
+    packed[packed_rows(dp, size) - 8 :] = jnp.zeros((packed.shape[0] - packed_rows(dp, size) + 8, size), f32)
     for i in range(dp):
         rows = nt(whole[i * size : (i + 1) * size], whole[i * size :])
-        for j in range(dp - i):
-            packed[at * size : (at + 1) * size] = rows[:, j * size : (j + 1) * size]
-            at += 1
-    if at * size < packed.shape[0]:
-        packed[at * size :] = jnp.zeros((packed.shape[0] - at * size, size), f32)
+        if i % 2 == 0:
+            even = rows[:, :size]
+        else:
+            pair = i // 2
+            packed[pair * size : (pair + 1) * size] = jnp.where(across >= down, even, rows[:, :size])
+            spare = packed_rows(dp, size) - 8 + pair
+            packed[spare : spare + 1] = jnp.sum(
+                jnp.where(across == down, rows[:, :size], 0.0), axis=0, keepdims=True
+            )
+        for j in range(1, dp - i):
+            packed[at : at + size] = rows[:, j * size : (j + 1) * size]
+            at += size
     count = packed.shape[0] // (nten * npre)
     for to, out in enumerate(outs):
         for by in range(npre):
@@ -105,14 +129,25 @@
     for at, piece in enumerate(pieces):
         packed[rows_at((ten ^ at // npre) * npre + (pre ^ at % npre), piece.shape[0])] = piece[...]
     total, width = normed.shape
-    size, at = total // dp, 0
+    size = total // dp
+    at = dp // 2 * size
+    down, across = positions(size)
     for i in range(dp):
-        for j in range(i, dp):
-            tile = packed[at * size : (at + 1) * size]
+        pair = i // 2
+        tile = packed[pair * size : (pair + 1) * size]
+        turned = tile.T
+        if i % 2 == 0:
+            tile = jnp.where(across >= down, tile, turned)
+        else:
+            spare = packed_rows(dp, size) - 8 + pair
+            tile = jnp.where(across < down, tile, turned)
+            tile = jnp.where(across == down, packed[spare : spare + 1], tile)
+        inner[i * size : (i + 1) * size, i * size : (i + 1) * size] = tile
+        for j in range(i + 1, dp):
+            tile = packed[at : at + size]
             inner[i * size : (i + 1) * size, j * size : (j + 1) * size] = tile
-            if j > i:
-                inner[j * size : (j + 1) * size, i * size : (i + 1) * size] = tile.T
-            at += 1
+            inner[j * size : (j + 1) * size, i * size : (i + 1) * size] = tile.T
+            at += size
     tokens_gram = high[...], low[...]
     both = inner[...] * (tokens_gram[0].astype(f32) + tokens_gram[1].astype(f32))
     power = jnp.sum(jnp.sum(both, axis=0, keepdims=True), axis=1, keepdims=True)
@@ -136,11 +171,23 @@
     root = lax.rsqrt(jnp.sqrt(scaling))
     value = halves(value * (0.25 * root))
     alone = (5.0 * base - damp * base * base * base * base * base) * 0.25 * root
-    made = nn(value[0], normed[...]) + nn(value[1], normed[...])
+    made = twice(value, normed[...])
     made = made + alone * output_rows(dp, nb, npre, me, pre, made.shape[0], width)
     each = outs[0].shape[0]
     for by, out in enumerate(outs):
         out[...] = made[by * each : (by + 1) * each]
+
+
+def place_kernel(nb, where, *refs):
+    parts, out, done = refs[:-2], refs[-2], refs[-1]
+    here = lax.rem(where[0], nb)
+    copies = [
+        pltpu.make_async_copy(part, out.at[here ^ by], done.at[by]) for by, part in enumerate(parts)
+    ]
+    for copy in copies:
+        copy.start()
+    for copy in copies:
+        copy.wait()
 
 
 def program(tokens, gain, cotangent):
@@ -152,15 +199,16 @@
     nb = width // BLK
     share = dp // nb
     assert nb * BLK == width and share * nb == dp
-    assert all(n & (n - 1) == 0 for n in (dp, nten, npre))
+    assert all(n & (n - 1) == 0 for n in (dp, nten, npre)) and 2 <= dp <= 16
     hidden = cotangent.shape[1] // (nten * dp)
     assert hidden * nten * dp == cotangent.shape[1]
 
     def cotangent_part(to):
         return lax.dynamic_slice_in_dim(cotangent, (ten * dp + to) * hidden, hidden, 1)
 
-    cotangents = [swap(cotangent_part(me ^ by).astype(f32), "dp", by) for by in range(1, dp)]
-    cotangents = [cotangent_part(me)] + cotangents
+    cotangents = [cotangent_part(me)]
+    for by in range(1, dp):
+        cotangents.append(swap(cotangent_part(me ^ by).astype(f32), "dp", by))
 
     values = tokens.astype(f32)
     square = jnp.sum(values * values, axis=1)[None, :]
@@ -173,12 +221,11 @@
         scale = lax.dynamic_slice_in_dim(gain, at, BLK, 0).astype(f32)
         return part * inverse * scale
 
-    normed_parts = [normed_part(me)]
+    normed_parts = [normed_part(me ^ by) for by in range(dp)]
     for by in range(1, dp):
-        normed_parts.append(swap(normed_part(me ^ by), "dp", by))
-
-    tiles = dp * (dp + 1) // 2
-    piece = -(-tiles * size // (nten * npre * 8)) * 8
+        normed_parts[by] = swap(normed_parts[by], "dp", by)
+
+    piece = -(-packed_rows(dp, size) // (nten * npre * 8)) * 8
     packed = pltpu.VMEM((nten * npre * piece, size), f32)
     part = jax.ShapeDtypeStruct((npre * piece, size), f32)
     parts = call(
@@ -187,7 +234,7 @@
         where,
         *cotangents,
         scratch=[pltpu.VMEM((total, hidden), bf16), packed],
-        flops=tiles * size * size * hidden * 2,
+        flops=total * total * hidden,
     )
     part = parts[0] + sum(swap(parts[to], "tensor", to) for to in range(1, nten))
     summed = part[:piece] + sum(
@@ -223,13 +270,23 @@
         scratch=[packed, pltpu.VMEM((total, total), f32)],
         flops=2 * total * total * (3 * total + 17 * made),
     )
-    result = jnp.zeros((nb, each, BLK), f32)
+    rows = list(rows)
     for by in range(nb):
         pairs = [(b * share + m, m * nb + (b ^ by)) for b in range(nb) for m in range(share)]
-        sent = rows[by]
         if any(a != b for a, b in pairs):
-            sent = lax.ppermute(sent, "dp", pairs)
-        result = lax.dynamic_update_slice_in_dim(result, sent[None], lax.rem(me, nb) ^ by, 0)
+            rows[by] = lax.ppermute(rows[by], "dp", pairs)
+    last = 1
+    (result,) = call(
+        functools.partial(place_kernel, nb),
+        [jax.ShapeDtypeStruct((nb, each, BLK), f32)],
+        where,
+        *rows[:last],
+        scratch=[pltpu.SemaphoreType.DMA((last,))],
+        vmem=4,
+        out_spec=ANY,
+    )
+    for by in range(last, nb):
+        result = lax.dynamic_update_slice_in_dim(result, rows[by][None], lax.rem(me, nb) ^ by, 0)
     return result
 
 

time: 88 us -> 88.2 us (level)
  Pallas kernels: 2.77 us -> 9.54 us
  local copies, waits for them, and re-layouts: 6.35 us -> 2.19 us
  waiting for transfers between devices: 51.9 us -> 49.2 us
    pallas_call x2 -> x4, Pallas kernels: 2.77 us -> 9.54 us  [call(): pl.pallas_call(kernel, out_shape=list(outs), in_specs=[SMEM] + [VMEM] * (...]
    pallas_call x1 -> x0, local copies, waits for them, and re-layouts: 5.45 us -> none  [call(): pl.pallas_call(kernel, out_shape=list(outs), in_specs=[SMEM] + [VMEM] * (...]
    ppermute x3, waiting for transfers between devices: 11.7 us -> 9.1 us  [program(): rows[by] = lax.ppermute(rows[by], 'dp', pairs)]
    dynamic_update_slice x3, local copies, waits for them, and re-layouts: 0.76 us -> 2.17 us  [program(): lax.dynamic_update_slice_in_dim(result, rows[by][None], lax.rem(me, nb) ^...]
  transfers between devices with their start and end apart: 24 -> 24, of which waited for: 14 -> 12; matrix products, arithmetic and copies ran while one was open for 1% -> 2% of each run, Pallas kernels for 3% -> 5%
where the time goes in v4:
time: 88.2 us; the launch traced here: 88.1 us
  waiting for transfers between devices  49.2 us (56%)
  starting transfers between devices  25 us (28%)
  Pallas kernels  9.54 us (11%)
  local copies, waits for them, and re-layouts  2.19 us (2%)
  other arithmetic  1.94 us (2%)
    ppermute x21, waiting for transfers between devices, swap(): return lax.ppermute(value, axis, [(i, i ^ by) for i in range(size)])  40.1 us
    ppermute x21, starting transfers between devices, swap(): return lax.ppermute(value, axis, [(i, i ^ by) for i in range(size)])  21.3 us
    pallas_call x4, Pallas kernels, call(): pl.pallas_call(kernel, out_shape=list(outs), in_specs=[SMEM] + [VMEM] * (...  9.54 us
    ppermute x3, waiting for transfers between devices, program(): rows[by] = lax.ppermute(rows[by], 'dp', pairs)  9.1 us
    ppermute x3, starting transfers between devices, program(): rows[by] = lax.ppermute(rows[by], 'dp', pairs)  3.62 us
    dynamic_update_slice x3, local copies, waits for them, and re-layouts, program(): lax.dynamic_update_slice_in_dim(result, rows[by][None], lax.rem(me, nb) ^...  2.17 us
  transfers between devices with their start and end apart: 24, of which 12 were waited for; matrix products, arithmetic and copies ran while one was open for 2% of the time, Pallas kernels for 5%

profile of v4, /device:TPU:0, one launch (start us, length us, event | category | flops | bytes accessed | tf_op | source)
XLA Modules:
  0.0 88.1 jit_solution(9954328765148911553)
XLA Ops:
  0.0 1.2 %dynamic-slice_convert_fusion = (f32[128,384]{1,0:T(8,128)S(1)}, f32[128,384]{1,0:T(8,128)S(1)}, bf16[128,384]{1,0:T(8,128)(2,1)S(1)}, f32[128,384]{1,0:T(8,128)S(1)}) fusion(bf16[128,3072]{1,0:T(8,128)(2,1)} %param.5, s32[]{:T(128)S(6)} %select_n.50, s32[]{:T(128)S(6)} %select_n.48, s32[]{:T(128)S(6)} %select_n.47, s32[]{:T(128)S(6)} %select_n.49), kind=kLoop, calls=%fused_computation.8 | loop fusion | flops 147456 | bytes 1081360 | tf_op jit(solution)/shard_map/convert_element_type | solution.py:211
  1.2 3.0 %collective-permute-start.4 = (f32[128,384]{1,0:T(8,128)S(1)}, f32[128,384]{1,0:T(8,128)S(1)}, u32[]{:S(2)}, u32[]{:S(2)}) collective-permute-start(f32[128,384]{1,0:T(8,128)S(1)} %get-tuple-element.30), channel_id=1, source_target_pairs={{0,8},{8,0},{16,24},{24,16},{1,9},{9,1},{17,25},{25,17},{2,10},{10... | collective-permute-start | bytes 589832 | tf_op jit(solution)/shard_map/ppermute | solution.py:25
  4.2 1.5 %collective-permute-start.5 = (f32[128,384]{1,0:T(8,128)S(1)}, f32[128,384]{1,0:T(8,128)S(1)}, u32[]{:S(2)}, u32[]{:S(2)}) collective-permute-start(f32[128,384]{1,0:T(8,128)S(1)} %get-tuple-element.32), channel_id=1, source_target_pairs={{0,16},{8,24},{16,0},{24,8},{1,17},{9,25},{17,1},{25,9},{2,18},{10... | collective-permute-start | bytes 589832 | tf_op jit(solution)/shard_map/ppermute | solution.py:25
  6.2 3.7 %collective-permute-done.4.refs_0_ = f32[128,384]{1,0:T(8,128)S(1)} collective-permute-done((f32[128,384]{1,0:T(8,128)S(1)}, f32[128,384]{1,0:T(8,128)S(1)}, u32[]{:S(2)}, u32[]{:S(2)}) %collective-permute-start.4) | collective-permute-done | bytes 196640 | tf_op jit(solution)/shard_map/ppermute | solution.py:25
  10.0 4.8 %collective-permute-done.5.refs_1_ = f32[128,384]{1,0:T(8,128)S(1)} collective-permute-done((f32[128,384]{1,0:T(8,128)S(1)}, f32[128,384]{1,0:T(8,128)S(1)}, u32[]{:S(2)}, u32[]{:S(2)}) %collective-permute-start.5) | collective-permute-done | bytes 196640 | tf_op jit(solution)/shard_map/ppermute | solution.py:25
  16.0 1.5 %collective-permute-done.7 = f32[544,128]{1,0:T(8,128)S(1)} collective-permute-done((f32[544,128]{1,0:T(8,128)S(1)}, f32[544,128]{1,0:T(8,128)S(1)}, u32[]{:S(2)}, u32[]{:S(2)}) %collective-permute-start.7) | collective-permute-done | bytes 278560 | tf_op jit(solution)/shard_map/ppermute | solution.py:25
  17.5 3.7 %collective-permute-start.10 = (f32[136,128]{1,0:T(8,128)S(1)}, f32[136,128]{1,0:T(8,128)S(1)}, u32[]{:S(2)}, u32[]{:S(2)}) collective-permute-start(f32[136,128]{1,0:T(8,128)S(1)} %get-tuple-element.34), channel_id=1, source_target_pairs={{0,3},{1,2},{2,1},{3,0},{4,7},{5,6},{6,5},{7,4},{8,11},{9,10},{10,... | collective-permute-start | bytes 208904 | tf_op jit(solution)/shard_map/ppermute | solution.py:25
  22.3 1.3 %collective-permute-start.1 = (f32[128,1024]{1,0:T(8,128)S(1)}, f32[128,1024]{1,0:T(8,128)S(1)}, u32[]{:S(2)}, u32[]{:S(2)}) collective-permute-start(f32[128,1024]{1,0:T(8,128)S(1)} %get-tuple-element.26), channel_id=1, source_target_pairs={{0,8},{8,0},{16,24},{24,16},{1,9},{9,1},{17,25},{25,17},{2,10},{10... | collective-permute-start | bytes 1572872 | tf_op jit(solution)/shard_map/ppermute | solution.py:25
  24.6 1.5 %collective-permute-start.3 = (f32[128,1024]{1,0:T(8,128)S(1)}, f32[128,1024]{1,0:T(8,128)S(1)}, u32[]{:S(2)}, u32[]{:S(2)}) collective-permute-start(f32[128,1024]{1,0:T(8,128)S(1)} %get-tuple-element.25), channel_id=1, source_target_pairs={{0,24},{8,16},{16,8},{24,0},{1,25},{9,17},{17,9},{25,1},{2,26},{10... | collective-permute-start | bytes 1572872 | tf_op jit(solution)/shard_map/ppermute | solution.py:25
  27.2 1.6 %collective-permute-start.13 = (f32[136,128]{1,0:T(8,128)S(1)}, f32[136,128]{1,0:T(8,128)S(1)}, u32[]{:S(2)}, u32[]{:S(2)}) collective-permute-start(f32[136,128]{1,0:T(8,128)S(1)} %slice_add_fusion), channel_id=1, source_target_pairs={{0,24},{8,16},{16,8},{24,0},{1,25},{9,17},{17,9},{25,1},{2,26},{10... | collective-permute-start | bytes 208904 | tf_op jit(solution)/shard_map/ppermute | solution.py:25
  28.8 1.5 %collective-permute-start.11 = (f32[136,128]{1,0:T(8,128)S(1)}, f32[136,128]{1,0:T(8,128)S(1)}, u32[]{:S(2)}, u32[]{:S(2)}) collective-permute-start(f32[136,128]{1,0:T(8,128)S(1)} %slice_add_fusion), channel_id=1, source_target_pairs={{0,8},{8,0},{16,24},{24,16},{1,9},{9,1},{17,25},{25,17},{2,10},{10... | collective-permute-start | bytes 208904 | tf_op jit(solution)/shard_map/ppermute | solution.py:25
  30.3 19.8 %collective-permute-done.13 = f32[136,128]{1,0:T(8,128)S(1)} collective-permute-done((f32[136,128]{1,0:T(8,128)S(1)}, f32[136,128]{1,0:T(8,128)S(1)}, u32[]{:S(2)}, u32[]{:S(2)}) %collective-permute-start.13) | collective-permute-done | bytes 69664 | tf_op jit(solution)/shard_map/ppermute | solution.py:25
  50.6 3.8 %collective-permute-done.12 = f32[136,128]{1,0:T(8,128)S(1)} collective-permute-done((f32[136,128]{1,0:T(8,128)S(1)}, f32[136,128]{1,0:T(8,128)S(1)}, u32[]{:S(2)}, u32[]{:S(2)}) %collective-permute-start.12) | collective-permute-done | bytes 69664 | tf_op jit(solution)/shard_map/ppermute | solution.py:25
  54.4 1.5 %collective-permute-start.14 = (f32[136,128]{1,0:T(8,128)S(1)}, f32[136,128]{1,0:T(8,128)S(1)}, u32[]{:S(2)}, u32[]{:S(2)}) collective-permute-start(f32[136,128]{1,0:T(8,128)S(1)} %add_add_fusion.refs_0_), channel_id=1, source_target_pairs={{0,1},{1,0},{2,3},{3,2},{4,5},{5,4},{6,7},{7,6},{8,9},{9,8},{10,11... | collective-permute-start | bytes 208904 | tf_op jit(solution)/shard_map/ppermute | solution.py:25
  55.9 2.6 %collective-permute-start.15 = (f32[136,128]{1,0:T(8,128)S(1)}, f32[136,128]{1,0:T(8,128)S(1)}, u32[]{:S(2)}, u32[]{:S(2)}) collective-permute-start(f32[136,128]{1,0:T(8,128)S(1)} %add_add_fusion.refs_0_), channel_id=1, source_target_pairs={{0,2},{1,3},{2,0},{3,1},{4,6},{5,7},{6,4},{7,5},{8,10},{9,11},{10,... | collective-permute-start | bytes 208904 | tf_op jit(solution)/shard_map/ppermute | solution.py:25
  59.4 2.4 %collective-permute-done.15.refs_2_ = f32[136,128]{1,0:T(8,128)S(1)} collective-permute-done((f32[136,128]{1,0:T(8,128)S(1)}, f32[136,128]{1,0:T(8,128)S(1)}, u32[]{:S(2)}, u32[]{:S(2)}) %collective-permute-start.15) | collective-permute-done | bytes 69664 | tf_op jit(solution)/shard_map/ppermute | solution.py:25
  61.8 2.8 %collective-permute-done.16.refs_3_ = f32[136,128]{1,0:T(8,128)S(1)} collective-permute-done((f32[136,128]{1,0:T(8,128)S(1)}, f32[136,128]{1,0:T(8,128)S(1)}, u32[]{:S(2)}, u32[]{:S(2)}) %collective-permute-start.16) | collective-permute-done | bytes 69664 | tf_op jit(solution)/shard_map/ppermute | solution.py:25
  64.6 1.7 %shard_map.37 = (bf16[512,1024]{1,0:T(8,128)(2,1)S(1)}, bf16[512,512]{1,0:T(8,128)(2,1)S(1)}, bf16[512,512]{1,0:T(8,128)(2,1)S(1)}, bf16[256,512]{1,0:T(8,128)(2,1)S(1)}) custom-call(s32[3]{0:T(128)S(1)} %pad_add_fusion.where, f32[128,1024]{1,0:T(8,128)S(1)} %get-tuple-element.27.own, f32[128,1024]{1,0:T(8,128)S(1)} %collective-permute-done.1.refs_0_, ...), custom_call_target="tpu_custom_call" | custom-call | flops 805306368 | bytes 4456460 | tf_op jit(solution)/shard_map/pallas_call | solution.py:30
  66.4 5.5 %shard_map.39 = (f32[64,1024]{1,0:T(8,128)S(1)}, f32[64,1024]{1,0:T(8,128)S(1)}, f32[64,1024]{1,0:T(8,128)S(1)}, f32[64,1024]{1,0:T(8,128)S(1)}) custom-call(s32[3]{0:T(128)S(1)} %pad_add_fusion.where, bf16[512,1024]{1,0:T(8,128)(2,1)S(1)} %get-tuple-element.15.normed, bf16[512,512]{1,0:T(8,128)(2,1)S(1)} %get-tuple-element.16.high, ...), custom_call_target="tpu_custom_call" | custom-call | flops 3087007744 | bytes 3964940 | tf_op jit(solution)/shard_map/pallas_call | solution.py:30
  72.6 1.2 %collective-permute-start.22 = (f32[64,1024]{1,0:T(8,128)S(1)}, f32[64,1024]{1,0:T(8,128)S(1)}, u32[]{:S(2)}, u32[]{:S(2)}) collective-permute-start(f32[64,1024]{1,0:T(8,128)S(1)} %get-tuple-element.23), channel_id=1, source_target_pairs={{0,16},{8,24},{16,0},{24,8},{1,17},{9,25},{17,1},{25,9},{2,18},{10... | collective-permute-start | bytes 786440 | tf_op jit(solution)/shard_map/ppermute | solution.py:277
  73.8 1.3 %shard_map.40 = f32[4,64,1024]{2,1,0:T(8,128)} custom-call(s32[3]{0:T(128)S(1)} %pad_add_fusion.where, f32[64,1024]{1,0:T(8,128)S(1)} %get-tuple-element.21.refs_0_), custom_call_target="tpu_custom_call" | custom-call | bytes 1310732 | tf_op jit(solution)/shard_map/pallas_call | solution.py:30
  75.1 1.8 %collective-permute-start.23 = (f32[64,1024]{1,0:T(8,128)S(1)}, f32[64,1024]{1,0:T(8,128)S(1)}, u32[]{:S(2)}, u32[]{:S(2)}) collective-permute-start(f32[64,1024]{1,0:T(8,128)S(1)} %get-tuple-element.24), channel_id=1, source_target_pairs={{0,24},{8,16},{16,8},{24,0},{1,25},{9,17},{17,9},{25,1},{2,26},{10... | collective-permute-start | bytes 786440 | tf_op jit(solution)/shard_map/ppermute | solution.py:277
  76.8 4.4 %collective-permute-done.21 = f32[64,1024]{1,0:T(8,128)S(1)} collective-permute-done((f32[64,1024]{1,0:T(8,128)S(1)}, f32[64,1024]{1,0:T(8,128)S(1)}, u32[]{:S(2)}, u32[]{:S(2)}) %collective-permute-start.21) | collective-permute-done | bytes 262176 | tf_op jit(solution)/shard_map/ppermute | solution.py:277
  81.9 4.7 %collective-permute-done.22 = f32[64,1024]{1,0:T(8,128)S(1)} collective-permute-done((f32[64,1024]{1,0:T(8,128)S(1)}, f32[64,1024]{1,0:T(8,128)S(1)}, u32[]{:S(2)}, u32[]{:S(2)}) %collective-permute-start.22) | collective-permute-done | bytes 262176 | tf_op jit(solution)/shard_map/ppermute | solution.py:277
  (45 shorter events, 9.1 us)
Async XLA Ops:
  1.2 8.8 %collective-permute-start.4 = (f32[128,384]{1,0:T(8,128)S(1)}, f32[128,384]{1,0:T(8,128)S(1)}, u32[]{:S(2)}, u32[]{:S(2)}) collective-permute-start(f32[128,384]{1,0:T(8,128)S(1)} %get-tuple-element.30), channel_id=1, source_target_pairs={{0,8},{8,0},{16,24},{24,16},{1,9},{9,1},{17,25},{25,17},{2,10},{10... | collective-permute-start | bytes 589832 | tf_op jit(solution)/shard_map/ppermute | solution.py:25
  4.2 10.6 %collective-permute-start.5 = (f32[128,384]{1,0:T(8,128)S(1)}, f32[128,384]{1,0:T(8,128)S(1)}, u32[]{:S(2)}, u32[]{:S(2)}) collective-permute-start(f32[128,384]{1,0:T(8,128)S(1)} %get-tuple-element.32), channel_id=1, source_target_pairs={{0,16},{8,24},{16,0},{24,8},{1,17},{9,25},{17,1},{25,9},{2,18},{10... | collective-permute-start | bytes 589832 | tf_op jit(solution)/shard_map/ppermute | solution.py:25
  5.7 9.1 %collective-permute-start.6 = (f32[128,384]{1,0:T(8,128)S(1)}, f32[128,384]{1,0:T(8,128)S(1)}, u32[]{:S(2)}, u32[]{:S(2)}) collective-permute-start(f32[128,384]{1,0:T(8,128)S(1)} %get-tuple-element.29), channel_id=1, source_target_pairs={{0,24},{8,16},{16,8},{24,0},{1,25},{9,17},{17,9},{25,1},{2,26},{10... | collective-permute-start | bytes 589832 | tf_op jit(solution)/shard_map/ppermute | solution.py:25
  6.1 9.9 %collective-permute-start = (f32[1,128]{1,0:T(1,128)S(1)}, f32[1,128]{1,0:T(1,128)S(1)}, u32[]{:S(2)}, u32[]{:S(2)}) collective-permute-start(f32[1,128]{1,0:T(1,128)S(1)} %bitcast.13), channel_id=1, source_target_pairs={{0,4},{4,0},{1,5},{5,1},{2,6},{6,2},{3,7},{7,3},{8,12},{12,8},{9,1... | collective-permute-start | bytes 1544 | tf_op jit(solution)/shard_map/ppermute | solution.py:25
  15.9 1.6 %collective-permute-start.7 = (f32[544,128]{1,0:T(8,128)S(1)}, f32[544,128]{1,0:T(8,128)S(1)}, u32[]{:S(2)}, u32[]{:S(2)}) collective-permute-start(f32[544,128]{1,0:T(8,128)S(1)} %get-tuple-element.20), channel_id=1, source_target_pairs={{0,4},{4,0},{1,5},{5,1},{2,6},{6,2},{3,7},{7,3},{8,12},{12,8},{9,1... | collective-permute-start | bytes 835592 | tf_op jit(solution)/shard_map/ppermute | solution.py:25
  17.5 7.0 %collective-permute-start.10 = (f32[136,128]{1,0:T(8,128)S(1)}, f32[136,128]{1,0:T(8,128)S(1)}, u32[]{:S(2)}, u32[]{:S(2)}) collective-permute-start(f32[136,128]{1,0:T(8,128)S(1)} %get-tuple-element.34), channel_id=1, source_target_pairs={{0,3},{1,2},{2,1},{3,0},{4,7},{5,6},{6,5},{7,4},{8,11},{9,10},{10,... | collective-permute-start | bytes 208904 | tf_op jit(solution)/shard_map/ppermute | solution.py:25
  21.2 5.2 %collective-permute-start.8 = (f32[136,128]{1,0:T(8,128)S(1)}, f32[136,128]{1,0:T(8,128)S(1)}, u32[]{:S(2)}, u32[]{:S(2)}) collective-permute-start(f32[136,128]{1,0:T(8,128)S(1)} %get-tuple-element.35), channel_id=1, source_target_pairs={{0,1},{1,0},{2,3},{3,2},{4,5},{5,4},{6,7},{7,6},{8,9},{9,8},{10,11... | collective-permute-start | bytes 208904 | tf_op jit(solution)/shard_map/ppermute | solution.py:25
  21.2 6.0 %collective-permute-start.9 = (f32[136,128]{1,0:T(8,128)S(1)}, f32[136,128]{1,0:T(8,128)S(1)}, u32[]{:S(2)}, u32[]{:S(2)}) collective-permute-start(f32[136,128]{1,0:T(8,128)S(1)} %get-tuple-element.33), channel_id=1, source_target_pairs={{0,2},{1,3},{2,0},{3,1},{4,6},{5,7},{6,4},{7,5},{8,10},{9,11},{10,... | collective-permute-start | bytes 208904 | tf_op jit(solution)/shard_map/ppermute | solution.py:25
  22.3 36.2 %collective-permute-start.1 = (f32[128,1024]{1,0:T(8,128)S(1)}, f32[128,1024]{1,0:T(8,128)S(1)}, u32[]{:S(2)}, u32[]{:S(2)}) collective-permute-start(f32[128,1024]{1,0:T(8,128)S(1)} %get-tuple-element.26), channel_id=1, source_target_pairs={{0,8},{8,0},{16,24},{24,16},{1,9},{9,1},{17,25},{25,17},{2,10},{10... | collective-permute-start | bytes 1572872 | tf_op jit(solution)/shard_map/ppermute | solution.py:25
  23.6 35.3 %collective-permute-start.2 = (f32[128,1024]{1,0:T(8,128)S(1)}, f32[128,1024]{1,0:T(8,128)S(1)}, u32[]{:S(2)}, u32[]{:S(2)}) collective-permute-start(f32[128,1024]{1,0:T(8,128)S(1)} %get-tuple-element.28), channel_id=1, source_target_pairs={{0,16},{8,24},{16,0},{24,8},{1,17},{9,25},{17,1},{25,9},{2,18},{10... | collective-permute-start | bytes 1572872 | tf_op jit(solution)/shard_map/ppermute | solution.py:25
  24.6 40.1 %collective-permute-start.3 = (f32[128,1024]{1,0:T(8,128)S(1)}, f32[128,1024]{1,0:T(8,128)S(1)}, u32[]{:S(2)}, u32[]{:S(2)}) collective-permute-start(f32[128,1024]{1,0:T(8,128)S(1)} %get-tuple-element.25), channel_id=1, source_target_pairs={{0,24},{8,16},{16,8},{24,0},{1,25},{9,17},{17,9},{25,1},{2,26},{10... | collective-permute-start | bytes 1572872 | tf_op jit(solution)/shard_map/ppermute | solution.py:25
  27.2 22.9 %collective-permute-start.13 = (f32[136,128]{1,0:T(8,128)S(1)}, f32[136,128]{1,0:T(8,128)S(1)}, u32[]{:S(2)}, u32[]{:S(2)}) collective-permute-start(f32[136,128]{1,0:T(8,128)S(1)} %slice_add_fusion), channel_id=1, source_target_pairs={{0,24},{8,16},{16,8},{24,0},{1,25},{9,17},{17,9},{25,1},{2,26},{10... | collective-permute-start | bytes 208904 | tf_op jit(solution)/shard_map/ppermute | solution.py:25
  28.8 21.9 %collective-permute-start.11 = (f32[136,128]{1,0:T(8,128)S(1)}, f32[136,128]{1,0:T(8,128)S(1)}, u32[]{:S(2)}, u32[]{:S(2)}) collective-permute-start(f32[136,128]{1,0:T(8,128)S(1)} %slice_add_fusion), channel_id=1, source_target_pairs={{0,8},{8,0},{16,24},{24,16},{1,9},{9,1},{17,25},{25,17},{2,10},{10... | collective-permute-start | bytes 208904 | tf_op jit(solution)/shard_map/ppermute | solution.py:25
  50.1 4.3 %collective-permute-start.12 = (f32[136,128]{1,0:T(8,128)S(1)}, f32[136,128]{1,0:T(8,128)S(1)}, u32[]{:S(2)}, u32[]{:S(2)}) collective-permute-start(f32[136,128]{1,0:T(8,128)S(1)} %slice_add_fusion), channel_id=1, source_target_pairs={{0,16},{8,24},{16,0},{24,8},{1,17},{9,25},{17,1},{25,9},{2,18},{10... | collective-permute-start | bytes 208904 | tf_op jit(solution)/shard_map/ppermute | solution.py:25
  54.4 4.5 %collective-permute-start.14 = (f32[136,128]{1,0:T(8,128)S(1)}, f32[136,128]{1,0:T(8,128)S(1)}, u32[]{:S(2)}, u32[]{:S(2)}) collective-permute-start(f32[136,128]{1,0:T(8,128)S(1)} %add_add_fusion.refs_0_), channel_id=1, source_target_pairs={{0,1},{1,0},{2,3},{3,2},{4,5},{5,4},{6,7},{7,6},{8,9},{9,8},{10,11... | collective-permute-start | bytes 208904 | tf_op jit(solution)/shard_map/ppermute | solution.py:25
  55.9 6.0 %collective-permute-start.15 = (f32[136,128]{1,0:T(8,128)S(1)}, f32[136,128]{1,0:T(8,128)S(1)}, u32[]{:S(2)}, u32[]{:S(2)}) collective-permute-start(f32[136,128]{1,0:T(8,128)S(1)} %add_add_fusion.refs_0_), channel_id=1, source_target_pairs={{0,2},{1,3},{2,0},{3,1},{4,6},{5,7},{6,4},{7,5},{8,10},{9,11},{10,... | collective-permute-start | bytes 208904 | tf_op jit(solution)/shard_map/ppermute | solution.py:25
  58.5 6.1 %collective-permute-start.16 = (f32[136,128]{1,0:T(8,128)S(1)}, f32[136,128]{1,0:T(8,128)S(1)}, u32[]{:S(2)}, u32[]{:S(2)}) collective-permute-start(f32[136,128]{1,0:T(8,128)S(1)} %add_add_fusion.refs_0_), channel_id=1, source_target_pairs={{0,3},{1,2},{2,1},{3,0},{4,7},{5,6},{6,5},{7,4},{8,11},{9,10},{10,... | collective-permute-start | bytes 208904 | tf_op jit(solution)/shard_map/ppermute | solution.py:25
  58.9 7.5 %collective-permute-start.17 = (f32[136,128]{1,0:T(8,128)S(1)}, f32[136,128]{1,0:T(8,128)S(1)}, u32[]{:S(2)}, u32[]{:S(2)}) collective-permute-start(f32[136,128]{1,0:T(8,128)S(1)} %add_add_fusion.refs_0_), channel_id=1, source_target_pairs={{0,4},{4,0},{1,5},{5,1},{2,6},{6,2},{3,7},{7,3},{8,12},{12,8},{9,1... | collective-permute-start | bytes 208904 | tf_op jit(solution)/shard_map/ppermute | solution.py:25
  58.9 7.5 %collective-permute-start.18 = (f32[136,128]{1,0:T(8,128)S(1)}, f32[136,128]{1,0:T(8,128)S(1)}, u32[]{:S(2)}, u32[]{:S(2)}) collective-permute-start(f32[136,128]{1,0:T(8,128)S(1)} %collective-permute-done.14.refs_1_), channel_id=1, source_target_pairs={{0,4},{4,0},{1,5},{5,1},{2,6},{6,2},{3,7},{7,3},{8,12},{12,8},{9,1... | collective-permute-start | bytes 208904 | tf_op jit(solution)/shard_map/ppermute | solution.py:25
  61.8 4.5 %collective-permute-start.19 = (f32[136,128]{1,0:T(8,128)S(1)}, f32[136,128]{1,0:T(8,128)S(1)}, u32[]{:S(2)}, u32[]{:S(2)}) collective-permute-start(f32[136,128]{1,0:T(8,128)S(1)} %collective-permute-done.15.refs_2_), channel_id=1, source_target_pairs={{0,4},{4,0},{1,5},{5,1},{2,6},{6,2},{3,7},{7,3},{8,12},{12,8},{9,1... | collective-permute-start | bytes 208904 | tf_op jit(solution)/shard_map/ppermute | solution.py:25
  64.6 1.8 %collective-permute-start.20 = (f32[136,128]{1,0:T(8,128)S(1)}, f32[136,128]{1,0:T(8,128)S(1)}, u32[]{:S(2)}, u32[]{:S(2)}) collective-permute-start(f32[136,128]{1,0:T(8,128)S(1)} %collective-permute-done.16.refs_3_), channel_id=1, source_target_pairs={{0,4},{4,0},{1,5},{5,1},{2,6},{6,2},{3,7},{7,3},{8,12},{12,8},{9,1... | collective-permute-start | bytes 208904 | tf_op jit(solution)/shard_map/ppermute | solution.py:25
  71.9 9.2 %collective-permute-start.21 = (f32[64,1024]{1,0:T(8,128)S(1)}, f32[64,1024]{1,0:T(8,128)S(1)}, u32[]{:S(2)}, u32[]{:S(2)}) collective-permute-start(f32[64,1024]{1,0:T(8,128)S(1)} %get-tuple-element.22), channel_id=1, source_target_pairs={{0,8},{8,0},{16,24},{24,16},{1,9},{9,1},{17,25},{25,17},{2,10},{10... | collective-permute-start | bytes 786440 | tf_op jit(solution)/shard_map/ppermute | solution.py:277
  72.6 14.0 %collective-permute-start.22 = (f32[64,1024]{1,0:T(8,128)S(1)}, f32[64,1024]{1,0:T(8,128)S(1)}, u32[]{:S(2)}, u32[]{:S(2)}) collective-permute-start(f32[64,1024]{1,0:T(8,128)S(1)} %get-tuple-element.23), channel_id=1, source_target_pairs={{0,16},{8,24},{16,0},{24,8},{1,17},{9,25},{17,1},{25,9},{2,18},{10... | collective-permute-start | bytes 786440 | tf_op jit(solution)/shard_map/ppermute | solution.py:277
  75.1 12.3 %collective-permute-start.23 = (f32[64,1024]{1,0:T(8,128)S(1)}, f32[64,1024]{1,0:T(8,128)S(1)}, u32[]{:S(2)}, u32[]{:S(2)}) collective-permute-start(f32[64,1024]{1,0:T(8,128)S(1)} %get-tuple-element.24), channel_id=1, source_target_pairs={{0,24},{8,16},{16,8},{24,0},{1,25},{9,17},{17,9},{25,1},{2,26},{10... | collective-permute-start | bytes 786440 | tf_op jit(solution)/shard_map/ppermute | solution.py:277
  (2 other events, 20.5 us)

commit v5 on v4

--- a/solution.py
+++ b/solution.py
@@ -20,8 +20,10 @@
 SMEM = pl.BlockSpec(memory_space=pltpu.SMEM)
 
 
-def swap(value, axis, by):
+def swap(value, axis, by, named=False):
     size = lax.axis_size(axis)
+    if named:
+        return swap(value, axis, by)
     return lax.ppermute(value, axis, [(i, i ^ by) for i in range(size)])
 
 
@@ -111,25 +113,34 @@
     return ((target * npre + pre) * each + lax.rem(made, each) == column).astype(f32)
 
 
-def normed_kernel(nb, npre, where, own, *refs):
+def early_kernel(dp, nb, npre, where, *refs):
     received, (normed, high, low, columns) = refs[:-4], refs[-4:]
-    me, pre = where[0], where[2]
-    size, dp = own.shape[0], len(received) + 1
-    normed[rows_at(me, size)] = own[...].astype(bf16)
-    for by, piece in enumerate(received, 1):
-        normed[rows_at(me ^ by, size)] = piece[...].astype(bf16)
+    size = received[0].shape[0]
+    for at, piece in enumerate(received):
+        normed[at * size : (at + 1) * size] = piece[...].astype(bf16)
     high[...], low[...] = halves(nt(normed[...], normed[...]))
-    select = output_rows(dp, nb, npre, me, pre, columns.shape[0], normed.shape[1])
+    select = output_rows(dp, nb, npre, where[0], where[2], columns.shape[0], normed.shape[1])
     columns[...] = nt(select.astype(bf16), normed[...]).astype(bf16)
 
 
-def root_kernel(dp, nb, npre, nten, where, normed, high, low, columns, *refs):
-    pieces, outs, packed, inner = refs[: nten * npre], refs[nten * npre : -2], refs[-2], refs[-1]
+def root_kernel(dp, nb, npre, nten, order, where, old, high, low, columns, *refs):
+    fresh = refs[: dp - old.shape[0] // refs[0].shape[0]]
+    refs = refs[len(fresh) :]
+    pieces, outs, (packed, inner, normed) = refs[: nten * npre], refs[nten * npre : -3], refs[-3:]
     me, ten, pre = where[0], where[1], where[2]
+    size, first = fresh[0].shape[0], old.shape[0]
+    total, width = normed.shape
+    normed[:first] = old[...]
+    for at, piece in enumerate(fresh):
+        normed[first + at * size : first + (at + 1) * size] = piece[...].astype(bf16)
     for at, piece in enumerate(pieces):
         packed[rows_at((ten ^ at // npre) * npre + (pre ^ at % npre), piece.shape[0])] = piece[...]
-    total, width = normed.shape
-    size = total // dp
+
+    def place(i):
+        return sum(jnp.where(me ^ i == by, at, 0) for at, by in enumerate(order))
+
+    places = [place(i) for i in range(dp)]
+    spot = [pl.ds(pl.multiple_of(at * size, size), size) for at in places]
     at = dp // 2 * size
     down, across = positions(size)
     for i in range(dp):
@@ -142,21 +153,30 @@
             spare = packed_rows(dp, size) - 8 + pair
             tile = jnp.where(across < down, tile, turned)
             tile = jnp.where(across == down, packed[spare : spare + 1], tile)
-        inner[i * size : (i + 1) * size, i * size : (i + 1) * size] = tile
+        inner[spot[i], spot[i]] = tile
         for j in range(i + 1, dp):
             tile = packed[at : at + size]
-            inner[i * size : (i + 1) * size, j * size : (j + 1) * size] = tile
-            inner[j * size : (j + 1) * size, i * size : (i + 1) * size] = tile.T
+            inner[spot[i], spot[j]] = tile
+            inner[spot[j], spot[i]] = tile.T
             at += size
-    tokens_gram = high[...], low[...]
+    select = output_rows(dp, nb, npre, me, pre, columns.shape[0], width)
+    later = normed[first:]
+    left = jnp.concatenate([columns[...], nt(select.astype(bf16), later).astype(bf16)], axis=1)
+    upper = halves(nt(normed[:first], later))
+    lower = halves(nt(later, normed[...]))
+    tokens_gram = [
+        jnp.concatenate([jnp.concatenate([one[...], two], axis=1), three], axis=0)
+        for one, two, three in zip((high, low), upper, lower)
+    ]
     both = inner[...] * (tokens_gram[0].astype(f32) + tokens_gram[1].astype(f32))
     power = jnp.sum(jnp.sum(both, axis=0, keepdims=True), axis=1, keepdims=True)
     scaling = 2.0 * (power / (float(total) * float(total)) / width + damping)
     damp = damping / scaling
     base = (5.0 - damp) / 4.0
-    core = halves(inner[...] * (1.0 / (scaling * (float(total) * float(total)))))
-    mixed = halves(product(tokens_gram, core))
-    rows = nn(columns[...], core[0]) + nn(columns[...], core[1])
+    scale = 1.0 / (scaling * (float(total) * float(total)))
+    core = halves(inner[...])
+    mixed = halves(product(tokens_gram, core) * scale)
+    rows = (nn(left, core[0]) + nn(left, core[1])) * scale
 
     def step(value, weight):
         return base * value - 0.25 * product(halves(value), mixed) + weight * rows
@@ -171,8 +191,7 @@
     root = lax.rsqrt(jnp.sqrt(scaling))
     value = halves(value * (0.25 * root))
     alone = (5.0 * base - damp * base * base * base * base * base) * 0.25 * root
-    made = twice(value, normed[...])
-    made = made + alone * output_rows(dp, nb, npre, me, pre, made.shape[0], width)
+    made = twice(value, normed[...]) + alone * select
     each = outs[0].shape[0]
     for by, out in enumerate(outs):
         out[...] = made[by * each : (by + 1) * each]
@@ -237,38 +256,38 @@
         flops=total * total * hidden,
     )
     part = parts[0] + sum(swap(parts[to], "tensor", to) for to in range(1, nten))
-    summed = part[:piece] + sum(
-        swap(part[by * piece : (by + 1) * piece], "precond", by) for by in range(1, npre)
-    )
+    summed = part[:piece] + sum(swap(part[by * piece : (by + 1) * piece], "precond", by, True) for by in range(1, npre))
     summed = summed + sum(swap(summed, "dp", by) for by in range(1, dp))
-    pieces = [summed] + [swap(summed, "precond", by) for by in range(1, npre)]
+    pieces = [summed] + [swap(summed, "precond", by, True) for by in range(1, npre)]
     pieces = pieces + [swap(one, "tensor", to) for to in range(1, nten) for one in pieces]
 
     each = BLK // (dp * npre)
     made = nb * each
-    normed, high, low, columns = call(
-        functools.partial(normed_kernel, nb, npre),
+    near = [by for by in range(1, dp) if by & (by - 1) == 0]
+    early = [by for by in range(dp) if by not in near]
+    first = len(early) * size
+    old = call(
+        functools.partial(early_kernel, dp, nb, npre),
         [
-            jax.ShapeDtypeStruct((total, BLK), bf16),
-            jax.ShapeDtypeStruct((total, total), bf16),
-            jax.ShapeDtypeStruct((total, total), bf16),
-            jax.ShapeDtypeStruct((made, total), bf16),
+            jax.ShapeDtypeStruct((first, BLK), bf16),
+            jax.ShapeDtypeStruct((first, first), bf16),
+            jax.ShapeDtypeStruct((first, first), bf16),
+            jax.ShapeDtypeStruct((made, first), bf16),
         ],
         where,
-        *normed_parts,
-        flops=2 * total * total * BLK + 2 * made * BLK * total,
+        *(normed_parts[by] for by in early),
+        flops=2 * first * first * BLK + 2 * made * BLK * first,
     )
     rows = call(
-        functools.partial(root_kernel, dp, nb, npre, nten),
+        functools.partial(root_kernel, dp, nb, npre, nten, early + near),
         [jax.ShapeDtypeStruct((each, BLK), f32)] * nb,
         where,
-        normed,
-        high,
-        low,
-        columns,
+        *old,
+        *(normed_parts[by] for by in near),
         *pieces,
-        scratch=[packed, pltpu.VMEM((total, total), f32)],
+        scratch=[packed, pltpu.VMEM((total, total), f32), pltpu.VMEM((total, BLK), bf16)],
         flops=2 * total * total * (3 * total + 17 * made),
+        vmem=20,
     )
     rows = list(rows)
     for by in range(nb):

time: 88.2 us -> 87.6 us (level)
  waiting for transfers between devices: 49.2 us -> 48.1 us
  starting transfers between devices: 25 us -> 26 us
    ppermute x21, starting transfers between devices: 21.3 us -> 22.4 us  [swap(): return lax.ppermute(value, axis, [(i, i ^ by) for i in range(size)])]
    ppermute x21, waiting for transfers between devices: 40.1 us -> 39.2 us  [swap(): return lax.ppermute(value, axis, [(i, i ^ by) for i in range(size)])]
  transfers between devices with their start and end apart: 24 -> 24, of which waited for: 12 -> 13; matrix products, arithmetic and copies ran while one was open for 2% -> 2% of each run, Pallas kernels for 5% -> 4%
where the time goes in v5:
time: 87.6 us; the launch traced here: 87.5 us
  waiting for transfers between devices  48.1 us (55%)
  starting transfers between devices  26 us (30%)
  Pallas kernels  9.03 us (10%)
  local copies, waits for them, and re-layouts  2.19 us (2%)
  other arithmetic  1.95 us (2%)
    ppermute x21, waiting for transfers between devices, swap(): return lax.ppermute(value, axis, [(i, i ^ by) for i in range(size)])  39.2 us
    ppermute x21, starting transfers between devices, swap(): return lax.ppermute(value, axis, [(i, i ^ by) for i in range(size)])  22.4 us
    pallas_call x4, Pallas kernels, call(): pl.pallas_call(kernel, out_shape=list(outs), in_specs=[SMEM] + [VMEM] * (...  9.03 us
    ppermute x3, waiting for transfers between devices, program(): rows[by] = lax.ppermute(rows[by], 'dp', pairs)  8.89 us
    ppermute x3, starting transfers between devices, program(): rows[by] = lax.ppermute(rows[by], 'dp', pairs)  3.62 us
    dynamic_update_slice x3, local copies, waits for them, and re-layouts, program(): lax.dynamic_update_slice_in_dim(result, rows[by][None], lax.rem(me, nb) ^...  2.17 us
  transfers between devices with their start and end apart: 24, of which 13 were waited for; matrix products, arithmetic and copies ran while one was open for 2% of the time, Pallas kernels for 4%

profile of v5, /device:TPU:0, one launch (start us, length us, event | category | flops | bytes accessed | tf_op | source)
XLA Modules:
  0.0 87.5 jit_solution(8850180584089711866)
XLA Ops:
  0.0 1.2 %dynamic-slice_convert_fusion = (f32[128,384]{1,0:T(8,128)S(1)}, f32[128,384]{1,0:T(8,128)S(1)}, bf16[128,384]{1,0:T(8,128)(2,1)S(1)}, f32[128,384]{1,0:T(8,128)S(1)}) fusion(bf16[128,3072]{1,0:T(8,128)(2,1)} %param.5, s32[]{:T(128)S(6)} %select_n.50, s32[]{:T(128)S(6)} %select_n.48, s32[]{:T(128)S(6)} %select_n.47, s32[]{:T(128)S(6)} %select_n.49), kind=kLoop, calls=%fused_computation.8 | loop fusion | flops 147456 | bytes 1081360 | tf_op jit(solution)/shard_map/convert_element_type | solution.py:230
  1.2 3.0 %collective-permute-start.4 = (f32[128,384]{1,0:T(8,128)S(1)}, f32[128,384]{1,0:T(8,128)S(1)}, u32[]{:S(2)}, u32[]{:S(2)}) collective-permute-start(f32[128,384]{1,0:T(8,128)S(1)} %get-tuple-element.30), channel_id=1, source_target_pairs={{0,8},{8,0},{16,24},{24,16},{1,9},{9,1},{17,25},{25,17},{2,10},{10... | collective-permute-start | bytes 589832 | tf_op jit(solution)/shard_map/ppermute | solution.py:27
  4.2 1.5 %collective-permute-start.5 = (f32[128,384]{1,0:T(8,128)S(1)}, f32[128,384]{1,0:T(8,128)S(1)}, u32[]{:S(2)}, u32[]{:S(2)}) collective-permute-start(f32[128,384]{1,0:T(8,128)S(1)} %get-tuple-element.32), channel_id=1, source_target_pairs={{0,16},{8,24},{16,0},{24,8},{1,17},{9,25},{17,1},{25,9},{2,18},{10... | collective-permute-start | bytes 589832 | tf_op jit(solution)/shard_map/ppermute | solution.py:27
  6.2 3.7 %collective-permute-done.4.refs_0_ = f32[128,384]{1,0:T(8,128)S(1)} collective-permute-done((f32[128,384]{1,0:T(8,128)S(1)}, f32[128,384]{1,0:T(8,128)S(1)}, u32[]{:S(2)}, u32[]{:S(2)}) %collective-permute-start.4) | collective-permute-done | bytes 196640 | tf_op jit(solution)/shard_map/ppermute | solution.py:27
  10.0 4.8 %collective-permute-done.5.refs_1_ = f32[128,384]{1,0:T(8,128)S(1)} collective-permute-done((f32[128,384]{1,0:T(8,128)S(1)}, f32[128,384]{1,0:T(8,128)S(1)}, u32[]{:S(2)}, u32[]{:S(2)}) %collective-permute-start.5) | collective-permute-done | bytes 196640 | tf_op jit(solution)/shard_map/ppermute | solution.py:27
  16.0 1.5 %collective-permute-done.7 = f32[544,128]{1,0:T(8,128)S(1)} collective-permute-done((f32[544,128]{1,0:T(8,128)S(1)}, f32[544,128]{1,0:T(8,128)S(1)}, u32[]{:S(2)}, u32[]{:S(2)}) %collective-permute-start.7) | collective-permute-done | bytes 278560 | tf_op jit(solution)/shard_map/ppermute | solution.py:27
  17.5 3.7 %collective-permute-start.10 = (f32[136,128]{1,0:T(8,128)S(1)}, f32[136,128]{1,0:T(8,128)S(1)}, u32[]{:S(2)}, u32[]{:S(2)}) collective-permute-start(f32[136,128]{1,0:T(8,128)S(1)} %get-tuple-element.34), channel_id=1, source_target_pairs={{0,3},{1,2},{2,1},{3,0},{4,7},{5,6},{6,5},{7,4},{8,11},{9,10},{10,... | collective-permute-start | bytes 208904 | tf_op jit(solution)/shard_map/ppermute | solution.py:27
  22.3 1.6 %collective-permute-start.1 = (f32[128,1024]{1,0:T(8,128)S(1)}, f32[128,1024]{1,0:T(8,128)S(1)}, u32[]{:S(2)}, u32[]{:S(2)}) collective-permute-start(f32[128,1024]{1,0:T(8,128)S(1)} %get-tuple-element.26), channel_id=1, source_target_pairs={{0,24},{8,16},{16,8},{24,0},{1,25},{9,17},{17,9},{25,1},{2,26},{10... | collective-permute-start | bytes 1572872 | tf_op jit(solution)/shard_map/ppermute | solution.py:27
  23.9 1.5 %collective-permute-start.2 = (f32[128,1024]{1,0:T(8,128)S(1)}, f32[128,1024]{1,0:T(8,128)S(1)}, u32[]{:S(2)}, u32[]{:S(2)}) collective-permute-start(f32[128,1024]{1,0:T(8,128)S(1)} %get-tuple-element.28), channel_id=1, source_target_pairs={{0,8},{8,0},{16,24},{24,16},{1,9},{9,1},{17,25},{25,17},{2,10},{10... | collective-permute-start | bytes 1572872 | tf_op jit(solution)/shard_map/ppermute | solution.py:27
  27.2 1.6 %collective-permute-start.13 = (f32[136,128]{1,0:T(8,128)S(1)}, f32[136,128]{1,0:T(8,128)S(1)}, u32[]{:S(2)}, u32[]{:S(2)}) collective-permute-start(f32[136,128]{1,0:T(8,128)S(1)} %slice_add_fusion), channel_id=1, source_target_pairs={{0,24},{8,16},{16,8},{24,0},{1,25},{9,17},{17,9},{25,1},{2,26},{10... | collective-permute-start | bytes 208904 | tf_op jit(solution)/shard_map/ppermute | solution.py:27
  28.8 1.5 %collective-permute-start.11 = (f32[136,128]{1,0:T(8,128)S(1)}, f32[136,128]{1,0:T(8,128)S(1)}, u32[]{:S(2)}, u32[]{:S(2)}) collective-permute-start(f32[136,128]{1,0:T(8,128)S(1)} %slice_add_fusion), channel_id=1, source_target_pairs={{0,8},{8,0},{16,24},{24,16},{1,9},{9,1},{17,25},{25,17},{2,10},{10... | collective-permute-start | bytes 208904 | tf_op jit(solution)/shard_map/ppermute | solution.py:27
  30.3 19.8 %collective-permute-done.13 = f32[136,128]{1,0:T(8,128)S(1)} collective-permute-done((f32[136,128]{1,0:T(8,128)S(1)}, f32[136,128]{1,0:T(8,128)S(1)}, u32[]{:S(2)}, u32[]{:S(2)}) %collective-permute-start.13) | collective-permute-done | bytes 69664 | tf_op jit(solution)/shard_map/ppermute | solution.py:27
  50.1 1.5 %collective-permute-start.12 = (f32[136,128]{1,0:T(8,128)S(1)}, f32[136,128]{1,0:T(8,128)S(1)}, u32[]{:S(2)}, u32[]{:S(2)}) collective-permute-start(f32[136,128]{1,0:T(8,128)S(1)} %slice_add_fusion), channel_id=1, source_target_pairs={{0,16},{8,24},{16,0},{24,8},{1,17},{9,25},{17,1},{25,9},{2,18},{10... | collective-permute-start | bytes 208904 | tf_op jit(solution)/shard_map/ppermute | solution.py:27
  51.6 2.8 %collective-permute-done.12 = f32[136,128]{1,0:T(8,128)S(1)} collective-permute-done((f32[136,128]{1,0:T(8,128)S(1)}, f32[136,128]{1,0:T(8,128)S(1)}, u32[]{:S(2)}, u32[]{:S(2)}) %collective-permute-start.12) | collective-permute-done | bytes 69664 | tf_op jit(solution)/shard_map/ppermute | solution.py:27
  54.4 1.5 %collective-permute-start.14 = (f32[136,128]{1,0:T(8,128)S(1)}, f32[136,128]{1,0:T(8,128)S(1)}, u32[]{:S(2)}, u32[]{:S(2)}) collective-permute-start(f32[136,128]{1,0:T(8,128)S(1)} %add_add_fusion.refs_2_), channel_id=1, source_target_pairs={{0,1},{1,0},{2,3},{3,2},{4,5},{5,4},{6,7},{7,6},{8,9},{9,8},{10,11... | collective-permute-start | bytes 208904 | tf_op jit(solution)/shard_map/ppermute | solution.py:27
  55.9 2.6 %collective-permute-start.15 = (f32[136,128]{1,0:T(8,128)S(1)}, f32[136,128]{1,0:T(8,128)S(1)}, u32[]{:S(2)}, u32[]{:S(2)}) collective-permute-start(f32[136,128]{1,0:T(8,128)S(1)} %add_add_fusion.refs_2_), channel_id=1, source_target_pairs={{0,2},{1,3},{2,0},{3,1},{4,6},{5,7},{6,4},{7,5},{8,10},{9,11},{10,... | collective-permute-start | bytes 208904 | tf_op jit(solution)/shard_map/ppermute | solution.py:27
  59.4 2.4 %collective-permute-done.15.refs_4_ = f32[136,128]{1,0:T(8,128)S(1)} collective-permute-done((f32[136,128]{1,0:T(8,128)S(1)}, f32[136,128]{1,0:T(8,128)S(1)}, u32[]{:S(2)}, u32[]{:S(2)}) %collective-permute-start.15) | collective-permute-done | bytes 69664 | tf_op jit(solution)/shard_map/ppermute | solution.py:27
  61.8 2.8 %collective-permute-done.16.refs_5_ = f32[136,128]{1,0:T(8,128)S(1)} collective-permute-done((f32[136,128]{1,0:T(8,128)S(1)}, f32[136,128]{1,0:T(8,128)S(1)}, u32[]{:S(2)}, u32[]{:S(2)}) %collective-permute-start.16) | collective-permute-done | bytes 69664 | tf_op jit(solution)/shard_map/ppermute | solution.py:27
  65.9 5.7 %shard_map.39 = (f32[64,1024]{1,0:T(8,128)S(1)}, f32[64,1024]{1,0:T(8,128)S(1)}, f32[64,1024]{1,0:T(8,128)S(1)}, f32[64,1024]{1,0:T(8,128)S(1)}) custom-call(s32[3]{0:T(128)S(1)} %pad_add_fusion.where, bf16[256,1024]{1,0:T(8,128)(2,1)S(1)} %get-tuple-element.15.old, bf16[256,256]{1,0:T(8,128)(2,1)S(1)} %get-tuple-element.16.high, ...), custom_call_target="tpu_custom_call" | custom-call | flops 3087007744 | bytes 3571724 | tf_op jit(solution)/shard_map/pallas_call | solution.py:32
  71.6 1.3 %collective-permute-start.21 = (f32[64,1024]{1,0:T(8,128)S(1)}, f32[64,1024]{1,0:T(8,128)S(1)}, u32[]{:S(2)}, u32[]{:S(2)}) collective-permute-start(f32[64,1024]{1,0:T(8,128)S(1)} %get-tuple-element.22), channel_id=1, source_target_pairs={{0,8},{8,0},{16,24},{24,16},{1,9},{9,1},{17,25},{25,17},{2,10},{10... | collective-permute-start | bytes 786440 | tf_op jit(solution)/shard_map/ppermute | solution.py:296
  73.7 1.3 %shard_map.40 = f32[4,64,1024]{2,1,0:T(8,128)} custom-call(s32[3]{0:T(128)S(1)} %pad_add_fusion.where, f32[64,1024]{1,0:T(8,128)S(1)} %get-tuple-element.21.refs_0_), custom_call_target="tpu_custom_call" | custom-call | bytes 1310732 | tf_op jit(solution)/shard_map/pallas_call | solution.py:32
  74.9 1.5 %collective-permute-start.23 = (f32[64,1024]{1,0:T(8,128)S(1)}, f32[64,1024]{1,0:T(8,128)S(1)}, u32[]{:S(2)}, u32[]{:S(2)}) collective-permute-start(f32[64,1024]{1,0:T(8,128)S(1)} %get-tuple-element.24), channel_id=1, source_target_pairs={{0,24},{8,16},{16,8},{24,0},{1,25},{9,17},{17,9},{25,1},{2,26},{10... | collective-permute-start | bytes 786440 | tf_op jit(solution)/shard_map/ppermute | solution.py:296
  76.4 4.4 %collective-permute-done.21 = f32[64,1024]{1,0:T(8,128)S(1)} collective-permute-done((f32[64,1024]{1,0:T(8,128)S(1)}, f32[64,1024]{1,0:T(8,128)S(1)}, u32[]{:S(2)}, u32[]{:S(2)}) %collective-permute-start.21) | collective-permute-done | bytes 262176 | tf_op jit(solution)/shard_map/ppermute | solution.py:296
  81.5 3.6 %collective-permute-done.22 = f32[64,1024]{1,0:T(8,128)S(1)} collective-permute-done((f32[64,1024]{1,0:T(8,128)S(1)}, f32[64,1024]{1,0:T(8,128)S(1)}, u32[]{:S(2)}, u32[]{:S(2)}) %collective-permute-start.22) | collective-permute-done | bytes 262176 | tf_op jit(solution)/shard_map/ppermute | solution.py:296
  (45 shorter events, 10.6 us)
Async XLA Ops:
  1.2 8.8 %collective-permute-start.4 = (f32[128,384]{1,0:T(8,128)S(1)}, f32[128,384]{1,0:T(8,128)S(1)}, u32[]{:S(2)}, u32[]{:S(2)}) collective-permute-start(f32[128,384]{1,0:T(8,128)S(1)} %get-tuple-element.30), channel_id=1, source_target_pairs={{0,8},{8,0},{16,24},{24,16},{1,9},{9,1},{17,25},{25,17},{2,10},{10... | collective-permute-start | bytes 589832 | tf_op jit(solution)/shard_map/ppermute | solution.py:27
  4.2 10.6 %collective-permute-start.5 = (f32[128,384]{1,0:T(8,128)S(1)}, f32[128,384]{1,0:T(8,128)S(1)}, u32[]{:S(2)}, u32[]{:S(2)}) collective-permute-start(f32[128,384]{1,0:T(8,128)S(1)} %get-tuple-element.32), channel_id=1, source_target_pairs={{0,16},{8,24},{16,0},{24,8},{1,17},{9,25},{17,1},{25,9},{2,18},{10... | collective-permute-start | bytes 589832 | tf_op jit(solution)/shard_map/ppermute | solution.py:27
  5.7 9.1 %collective-permute-start.6 = (f32[128,384]{1,0:T(8,128)S(1)}, f32[128,384]{1,0:T(8,128)S(1)}, u32[]{:S(2)}, u32[]{:S(2)}) collective-permute-start(f32[128,384]{1,0:T(8,128)S(1)} %get-tuple-element.29), channel_id=1, source_target_pairs={{0,24},{8,16},{16,8},{24,0},{1,25},{9,17},{17,9},{25,1},{2,26},{10... | collective-permute-start | bytes 589832 | tf_op jit(solution)/shard_map/ppermute | solution.py:27
  6.1 9.9 %collective-permute-start = (f32[1,128]{1,0:T(1,128)S(1)}, f32[1,128]{1,0:T(1,128)S(1)}, u32[]{:S(2)}, u32[]{:S(2)}) collective-permute-start(f32[1,128]{1,0:T(1,128)S(1)} %bitcast.13), channel_id=1, source_target_pairs={{0,4},{4,0},{1,5},{5,1},{2,6},{6,2},{3,7},{7,3},{8,12},{12,8},{9,1... | collective-permute-start | bytes 1544 | tf_op jit(solution)/shard_map/ppermute | solution.py:27
  15.9 1.6 %collective-permute-start.7 = (f32[544,128]{1,0:T(8,128)S(1)}, f32[544,128]{1,0:T(8,128)S(1)}, u32[]{:S(2)}, u32[]{:S(2)}) collective-permute-start(f32[544,128]{1,0:T(8,128)S(1)} %get-tuple-element.20), channel_id=1, source_target_pairs={{0,4},{4,0},{1,5},{5,1},{2,6},{6,2},{3,7},{7,3},{8,12},{12,8},{9,1... | collective-permute-start | bytes 835592 | tf_op jit(solution)/shard_map/ppermute | solution.py:27
  17.5 7.8 %collective-permute-start.10 = (f32[136,128]{1,0:T(8,128)S(1)}, f32[136,128]{1,0:T(8,128)S(1)}, u32[]{:S(2)}, u32[]{:S(2)}) collective-permute-start(f32[136,128]{1,0:T(8,128)S(1)} %get-tuple-element.34), channel_id=1, source_target_pairs={{0,3},{1,2},{2,1},{3,0},{4,7},{5,6},{6,5},{7,4},{8,11},{9,10},{10,... | collective-permute-start | bytes 208904 | tf_op jit(solution)/shard_map/ppermute | solution.py:27
  21.2 5.2 %collective-permute-start.8 = (f32[136,128]{1,0:T(8,128)S(1)}, f32[136,128]{1,0:T(8,128)S(1)}, u32[]{:S(2)}, u32[]{:S(2)}) collective-permute-start(f32[136,128]{1,0:T(8,128)S(1)} %get-tuple-element.35), channel_id=1, source_target_pairs={{0,1},{1,0},{2,3},{3,2},{4,5},{5,4},{6,7},{7,6},{8,9},{9,8},{10,11... | collective-permute-start | bytes 208904 | tf_op jit(solution)/shard_map/ppermute | solution.py:27
  21.2 6.0 %collective-permute-start.9 = (f32[136,128]{1,0:T(8,128)S(1)}, f32[136,128]{1,0:T(8,128)S(1)}, u32[]{:S(2)}, u32[]{:S(2)}) collective-permute-start(f32[136,128]{1,0:T(8,128)S(1)} %get-tuple-element.33), channel_id=1, source_target_pairs={{0,2},{1,3},{2,0},{3,1},{4,6},{5,7},{6,4},{7,5},{8,10},{9,11},{10,... | collective-permute-start | bytes 208904 | tf_op jit(solution)/shard_map/ppermute | solution.py:27
  22.3 36.2 %collective-permute-start.1 = (f32[128,1024]{1,0:T(8,128)S(1)}, f32[128,1024]{1,0:T(8,128)S(1)}, u32[]{:S(2)}, u32[]{:S(2)}) collective-permute-start(f32[128,1024]{1,0:T(8,128)S(1)} %get-tuple-element.26), channel_id=1, source_target_pairs={{0,24},{8,16},{16,8},{24,0},{1,25},{9,17},{17,9},{25,1},{2,26},{10... | collective-permute-start | bytes 1572872 | tf_op jit(solution)/shard_map/ppermute | solution.py:27
  23.9 35.0 %collective-permute-start.2 = (f32[128,1024]{1,0:T(8,128)S(1)}, f32[128,1024]{1,0:T(8,128)S(1)}, u32[]{:S(2)}, u32[]{:S(2)}) collective-permute-start(f32[128,1024]{1,0:T(8,128)S(1)} %get-tuple-element.28), channel_id=1, source_target_pairs={{0,8},{8,0},{16,24},{24,16},{1,9},{9,1},{17,25},{25,17},{2,10},{10... | collective-permute-start | bytes 1572872 | tf_op jit(solution)/shard_map/ppermute | solution.py:27
  25.4 40.3 %collective-permute-start.3 = (f32[128,1024]{1,0:T(8,128)S(1)}, f32[128,1024]{1,0:T(8,128)S(1)}, u32[]{:S(2)}, u32[]{:S(2)}) collective-permute-start(f32[128,1024]{1,0:T(8,128)S(1)} %get-tuple-element.25), channel_id=1, source_target_pairs={{0,16},{8,24},{16,0},{24,8},{1,17},{9,25},{17,1},{25,9},{2,18},{10... | collective-permute-start | bytes 1572872 | tf_op jit(solution)/shard_map/ppermute | solution.py:27
  27.2 22.9 %collective-permute-start.13 = (f32[136,128]{1,0:T(8,128)S(1)}, f32[136,128]{1,0:T(8,128)S(1)}, u32[]{:S(2)}, u32[]{:S(2)}) collective-permute-start(f32[136,128]{1,0:T(8,128)S(1)} %slice_add_fusion), channel_id=1, source_target_pairs={{0,24},{8,16},{16,8},{24,0},{1,25},{9,17},{17,9},{25,1},{2,26},{10... | collective-permute-start | bytes 208904 | tf_op jit(solution)/shard_map/ppermute | solution.py:27
  28.8 22.8 %collective-permute-start.11 = (f32[136,128]{1,0:T(8,128)S(1)}, f32[136,128]{1,0:T(8,128)S(1)}, u32[]{:S(2)}, u32[]{:S(2)}) collective-permute-start(f32[136,128]{1,0:T(8,128)S(1)} %slice_add_fusion), channel_id=1, source_target_pairs={{0,8},{8,0},{16,24},{24,16},{1,9},{9,1},{17,25},{25,17},{2,10},{10... | collective-permute-start | bytes 208904 | tf_op jit(solution)/shard_map/ppermute | solution.py:27
  50.1 4.3 %collective-permute-start.12 = (f32[136,128]{1,0:T(8,128)S(1)}, f32[136,128]{1,0:T(8,128)S(1)}, u32[]{:S(2)}, u32[]{:S(2)}) collective-permute-start(f32[136,128]{1,0:T(8,128)S(1)} %slice_add_fusion), channel_id=1, source_target_pairs={{0,16},{8,24},{16,0},{24,8},{1,17},{9,25},{17,1},{25,9},{2,18},{10... | collective-permute-start | bytes 208904 | tf_op jit(solution)/shard_map/ppermute | solution.py:27
  54.4 4.5 %collective-permute-start.14 = (f32[136,128]{1,0:T(8,128)S(1)}, f32[136,128]{1,0:T(8,128)S(1)}, u32[]{:S(2)}, u32[]{:S(2)}) collective-permute-start(f32[136,128]{1,0:T(8,128)S(1)} %add_add_fusion.refs_2_), channel_id=1, source_target_pairs={{0,1},{1,0},{2,3},{3,2},{4,5},{5,4},{6,7},{7,6},{8,9},{9,8},{10,11... | collective-permute-start | bytes 208904 | tf_op jit(solution)/shard_map/ppermute | solution.py:27
  55.9 6.0 %collective-permute-start.15 = (f32[136,128]{1,0:T(8,128)S(1)}, f32[136,128]{1,0:T(8,128)S(1)}, u32[]{:S(2)}, u32[]{:S(2)}) collective-permute-start(f32[136,128]{1,0:T(8,128)S(1)} %add_add_fusion.refs_2_), channel_id=1, source_target_pairs={{0,2},{1,3},{2,0},{3,1},{4,6},{5,7},{6,4},{7,5},{8,10},{9,11},{10,... | collective-permute-start | bytes 208904 | tf_op jit(solution)/shard_map/ppermute | solution.py:27
  58.5 6.1 %collective-permute-start.16 = (f32[136,128]{1,0:T(8,128)S(1)}, f32[136,128]{1,0:T(8,128)S(1)}, u32[]{:S(2)}, u32[]{:S(2)}) collective-permute-start(f32[136,128]{1,0:T(8,128)S(1)} %add_add_fusion.refs_2_), channel_id=1, source_target_pairs={{0,3},{1,2},{2,1},{3,0},{4,7},{5,6},{6,5},{7,4},{8,11},{9,10},{10,... | collective-permute-start | bytes 208904 | tf_op jit(solution)/shard_map/ppermute | solution.py:27
  58.9 6.8 %collective-permute-start.17 = (f32[136,128]{1,0:T(8,128)S(1)}, f32[136,128]{1,0:T(8,128)S(1)}, u32[]{:S(2)}, u32[]{:S(2)}) collective-permute-start(f32[136,128]{1,0:T(8,128)S(1)} %add_add_fusion.refs_2_), channel_id=1, source_target_pairs={{0,4},{4,0},{1,5},{5,1},{2,6},{6,2},{3,7},{7,3},{8,12},{12,8},{9,1... | collective-permute-start | bytes 208904 | tf_op jit(solution)/shard_map/ppermute | solution.py:27
  58.9 6.8 %collective-permute-start.18 = (f32[136,128]{1,0:T(8,128)S(1)}, f32[136,128]{1,0:T(8,128)S(1)}, u32[]{:S(2)}, u32[]{:S(2)}) collective-permute-start(f32[136,128]{1,0:T(8,128)S(1)} %collective-permute-done.14.refs_3_), channel_id=1, source_target_pairs={{0,4},{4,0},{1,5},{5,1},{2,6},{6,2},{3,7},{7,3},{8,12},{12,8},{9,1... | collective-permute-start | bytes 208904 | tf_op jit(solution)/shard_map/ppermute | solution.py:27
  61.8 3.9 %collective-permute-start.19 = (f32[136,128]{1,0:T(8,128)S(1)}, f32[136,128]{1,0:T(8,128)S(1)}, u32[]{:S(2)}, u32[]{:S(2)}) collective-permute-start(f32[136,128]{1,0:T(8,128)S(1)} %collective-permute-done.15.refs_4_), channel_id=1, source_target_pairs={{0,4},{4,0},{1,5},{5,1},{2,6},{6,2},{3,7},{7,3},{8,12},{12,8},{9,1... | collective-permute-start | bytes 208904 | tf_op jit(solution)/shard_map/ppermute | solution.py:27
  64.6 1.3 %collective-permute-start.20 = (f32[136,128]{1,0:T(8,128)S(1)}, f32[136,128]{1,0:T(8,128)S(1)}, u32[]{:S(2)}, u32[]{:S(2)}) collective-permute-start(f32[136,128]{1,0:T(8,128)S(1)} %collective-permute-done.16.refs_5_), channel_id=1, source_target_pairs={{0,4},{4,0},{1,5},{5,1},{2,6},{6,2},{3,7},{7,3},{8,12},{12,8},{9,1... | collective-permute-start | bytes 208904 | tf_op jit(solution)/shard_map/ppermute | solution.py:27
  71.6 9.2 %collective-permute-start.21 = (f32[64,1024]{1,0:T(8,128)S(1)}, f32[64,1024]{1,0:T(8,128)S(1)}, u32[]{:S(2)}, u32[]{:S(2)}) collective-permute-start(f32[64,1024]{1,0:T(8,128)S(1)} %get-tuple-element.22), channel_id=1, source_target_pairs={{0,8},{8,0},{16,24},{24,16},{1,9},{9,1},{17,25},{25,17},{2,10},{10... | collective-permute-start | bytes 786440 | tf_op jit(solution)/shard_map/ppermute | solution.py:296
  72.9 12.3 %collective-permute-start.22 = (f32[64,1024]{1,0:T(8,128)S(1)}, f32[64,1024]{1,0:T(8,128)S(1)}, u32[]{:S(2)}, u32[]{:S(2)}) collective-permute-start(f32[64,1024]{1,0:T(8,128)S(1)} %get-tuple-element.23), channel_id=1, source_target_pairs={{0,16},{8,24},{16,0},{24,8},{1,17},{9,25},{17,1},{25,9},{2,18},{10... | collective-permute-start | bytes 786440 | tf_op jit(solution)/shard_map/ppermute | solution.py:296
  74.9 11.8 %collective-permute-start.23 = (f32[64,1024]{1,0:T(8,128)S(1)}, f32[64,1024]{1,0:T(8,128)S(1)}, u32[]{:S(2)}, u32[]{:S(2)}) collective-permute-start(f32[64,1024]{1,0:T(8,128)S(1)} %get-tuple-element.24), channel_id=1, source_target_pairs={{0,24},{8,16},{16,8},{24,0},{1,25},{9,17},{17,9},{25,1},{2,26},{10... | collective-permute-start | bytes 786440 | tf_op jit(solution)/shard_map/ppermute | solution.py:296
  (2 other events, 20.5 us)
